TPU v7x, 256 devices: a whole 4x4x8 slice. The times are simulated.
256 devices in a mesh: dp: 2 (over core), expert: 8 (over z), ffn: 16 (over y, x).
Axes of the slice: x: 4, y: 4, z: 8, core: 2. Of those that a mesh axis runs over, the one named last changes fastest.
Arguments:
- tokens: bfloat16 [2048, 6144], P(('dp', 'expert'), 'ffn'), may hold values from -6 to 6
- routes: int32 [2048, 2], P(('dp', 'expert')), may hold values from 0 to 7, all different within a row; in each aligned block of 128 rows (0 to 127, 128 to 255, ...) at most 64 rows name the same one
- keep: int32 [16, 8], P(('dp', 'expert')), may hold values from 0 to 1, as said below
- router: float32 [6144, 8], P('ffn'), may hold values from -0.078125 to 0.078125
- w_gate: bfloat16 [8, 6144, 8192], P('expert', None, ('dp', 'ffn')), may hold values from -0.078125 to 0.078125
- w_up: bfloat16 [8, 6144, 8192], P('expert', None, ('dp', 'ffn')), may hold values from -0.078125 to 0.078125
- w_down: bfloat16 [8, 8192, 6144], P('expert', ('dp', 'ffn')), may hold values from -0.125 to 0.125
Outputs:
- full_out: bfloat16 [2048, 6144], P(('dp', 'expert'), 'ffn')
- pruned_out: bfloat16 [2048, 6144], P(('dp', 'expert'), 'ffn')
- residual: float32 [2048, 6144], P(('dp', 'expert'), 'ffn')
- router_grad: float32 [6144, 8], P('ffn')
Inputs may be any that keep to these rules, and one draw needn't show every extreme that they name: `routes`: each row names two different experts; in the 128 rows of one block no expert is named by more than 64 rows, a bound that some block reaches. `keep`: in every row between 2 and 4 entries are 0, the others 1.
All inputs are finite; a program needn't handle non-finite values.
Results may differ from a plain program's by a relative error of at most 0.02.
Values may be sent and summed in bfloat16 or wider, within the bound.
A program may use at most 128 MiB of HBM per device.

v0:
```python
import jax
import jax.numpy as jnp
from jax import lax
from jax.sharding import PartitionSpec as P


def from_everyone(shard, axis):
    length = lax.axis_size(axis)
    return lax.all_to_all(
        jnp.broadcast_to(shard[None], (length, *shard.shape)), axis, 0, 0, tiled=True
    )


def taken_together(shard, axis):
    return from_everyone(shard, axis).sum(axis=0)


def slot_numbers(routes, experts):
    flat = routes.reshape(-1)
    onehot = (flat[:, None] == jnp.arange(experts, dtype=jnp.int32)[None, :]).astype(jnp.int32)
    before = jnp.cumsum(onehot, axis=0) - onehot
    return jnp.sum(before * onehot, axis=1).reshape(routes.shape)


def on_device(tokens, routes, keep, router, w_gate, w_up, w_down):
    experts = keep.shape[1]
    tok_rows = tokens.shape[0]
    capacity = tok_rows // 2
    slots = slot_numbers(routes, experts)
    target = routes * capacity + slots
    positions = jnp.arange(experts * capacity, dtype=jnp.int32)
    send_map = jnp.logical_or(
        positions[:, None] == target[None, :, 0], positions[:, None] == target[None, :, 1]
    ).astype(jnp.bfloat16)
    pick_first = (target[:, 0:1] == positions[None, :]).astype(jnp.bfloat16)
    pick_second = (target[:, 1:2] == positions[None, :]).astype(jnp.bfloat16)
    gate_w = w_gate[0]
    up_w = w_up[0]
    down_w = w_down[0]
    local_logits = jnp.dot(tokens.astype(jnp.float32), router, precision=lax.Precision.HIGHEST)
    logits = taken_together(local_logits, "ffn")
    outgoing = jnp.dot(send_map, tokens, preferred_element_type=jnp.float32).astype(jnp.bfloat16)
    arrived = lax.all_to_all(outgoing, "expert", split_axis=0, concat_axis=0, tiled=True)
    slot_rows = lax.all_gather(arrived, "dp", axis=0, tiled=True)
    piece = lax.all_gather(slot_rows, "ffn", axis=1, tiled=True)
    gate = jnp.dot(piece, gate_w, preferred_element_type=jnp.float32)
    up = jnp.dot(piece, up_w, preferred_element_type=jnp.float32)
    hidden = (jax.nn.silu(gate) * up).astype(jnp.bfloat16)
    n_cores = lax.axis_size("dp")
    n_slices = lax.axis_size("ffn")
    per_core = hidden.shape[0] // n_cores
    slice_width = down_w.shape[1] // n_slices
    split_hidden = hidden.reshape(n_cores, per_core, hidden.shape[1])
    split_down = down_w.reshape(down_w.shape[0], n_slices, slice_width)
    terms = jnp.einsum(
        "cri,ifd->cfrd", split_hidden, split_down, preferred_element_type=jnp.float32
    )
    terms = terms.reshape(n_cores * n_slices * per_core, slice_width)
    summed = lax.psum_scatter(
        terms.astype(jnp.bfloat16), ("dp", "ffn"), scatter_dimension=0, tiled=True
    )
    returned = lax.all_to_all(summed, "expert", split_axis=0, concat_axis=0, tiled=True)
    first = jnp.dot(pick_first, returned, preferred_element_type=jnp.float32)
    second = jnp.dot(pick_second, returned, preferred_element_type=jnp.float32)
    expert_ids = jnp.arange(experts, dtype=jnp.int32)[None, :]
    onehot_first = (routes[:, 0:1] == expert_ids).astype(jnp.float32)
    onehot_second = (routes[:, 1:2] == expert_ids).astype(jnp.float32)
    keep_f = keep[0].astype(jnp.float32)[None, :]
    keep_first = jnp.sum(onehot_first * keep_f, axis=1)
    keep_second = jnp.sum(onehot_second * keep_f, axis=1)
    diff = jnp.sum(onehot_first * logits, axis=1) - jnp.sum(onehot_second * logits, axis=1)
    share = jax.nn.sigmoid(diff)
    other = jax.nn.sigmoid(-diff)
    pruned_first = keep_first * (keep_second * share + 1.0 - keep_second)
    pruned_second = keep_second * (keep_first * other + 1.0 - keep_first)
    full32 = share[:, None] * first + other[:, None] * second
    pruned32 = pruned_first[:, None] * first + pruned_second[:, None] * second
    residual = full32 - pruned32
    inner = taken_together(jnp.sum(residual * (first - second), axis=1), "ffn")
    slope = share * (1.0 - share) * (1.0 - keep_first * keep_second) * inner
    grad_logits = onehot_first * slope[:, None] - onehot_second * slope[:, None]
    local_grad = jnp.dot(tokens.astype(jnp.float32).T, grad_logits, precision=lax.Precision.HIGHEST)
    router_grad = taken_together(local_grad, ("dp", "expert"))
    return (full32.astype(jnp.bfloat16), pruned32.astype(jnp.bfloat16), residual, router_grad)


def solution(mesh):
    return jax.shard_map(
        on_device,
        mesh=mesh,
        in_specs=(
            P(("dp", "expert"), "ffn"),
            P(("dp", "expert"), None),
            P(("dp", "expert"), None),
            P("ffn", None),
            P("expert", None, ("dp", "ffn")),
            P("expert", None, ("dp", "ffn")),
            P("expert", ("dp", "ffn"), None),
        ),
        out_specs=(
            P(("dp", "expert"), "ffn"),
            P(("dp", "expert"), "ffn"),
            P(("dp", "expert"), "ffn"),
            P("ffn", None),
        ),
        check_vma=False,
    )
```

profile of v0, /device:TPU:1, one launch (start us, length us, event | category | flops | bytes accessed | tf_op | source)
XLA Modules:
  0.0 324.0 jit_solution(17251408509211322227)
XLA Ops:
  7.2 0.9 copy.49
  8.5 0.6 reduce-window.6
  9.0 0.2 slice_reduce_fusion
  9.6 0.7 multiply_add_fusion.2
  10.3 1.2 convolution_convert_fusion.1
  11.5 22.4 %all_to_all.40 = bf16[8,64,384]{2,1,0:T(8,128)(2,1)S(1)} all-to-all(bf16[8,64,384]{2,1,0:T(8,128)(2,1)S(1)} %bitcast.64), channel_id=1, replica_groups=mesh['dp'=2,'expert'=8,'ffn'=16] {'expert'}, dimensions={0} | all-to-all | bytes 786432 | tf_op jit(solution)/shard_map/all_to_all | solution.py:43
  33.9 4.2 %all_gather.6 = bf16[1024,384]{1,0:T(8,128)(2,1)} all-gather(bf16[512,384]{1,0:T(8,128)(2,1)S(1)} %bitcast.63), channel_id=1, replica_groups=mesh['dp'=2,'expert'=8,'ffn'=16] {'dp'}, dimensions={0}, use_global_device_ids=true | all-gather | bytes 1179648 | tf_op jit(solution)/shard_map/all_gather | solution.py:44
  38.1 4.2 %copy.55 = bf16[32,8,16,384]{3,2,1,0:T(8,128)(2,1)} copy(bf16[32,8,16,384]{3,1,2,0:T(8,128)(2,1)} %bitcast.62) | data formatting | bytes 6291456
  42.4 94.0 %all-gather.2.cloned.1.call-done = bf16[1024,6144]{1,0:T(8,128)(2,1)} async-done(((bf16[1024,384]{1,0:T(8,128)(2,1)}), bf16[1024,6144]{1,0:T(8,128)(2,1)}) %all-gather.2.cloned.1.call-update) | async-done | bytes 12582928 | tf_op jit(solution)/shard_map/all_gather | solution.py:45
  136.4 7.7 %fusion.3 = f32[1024,256]{1,0:T(8,128)S(1)} fusion(bf16[1024,6144]{1,0:T(8,128)(2,1)} %all-gather.2.cloned.1.call-done, bf16[1,6144,256]{2,1,0:T(8,128)(2,1)S(1)} %copy-done), kind=kOutput, calls=%fused_computation.4 | convolution fusion | flops 3221225472 | bytes 16777216 | tf_op jit(solution)/shard_map/dot_general | solution.py:46
  144.1 0.5 copy-done.8
  144.6 0.9 copy-done.9
  145.5 3.4 %fusion.9 = bf16[1024,256]{1,0:T(8,128)(2,1)S(1)} fusion(bf16[1024,6144]{1,0:T(8,128)(2,1)S(1)} %copy-done.8, bf16[1,6144,256]{2,1,0:T(8,128)(2,1)S(1)} %copy-done.9, f32[1024,256]{1,0:T(8,128)S(1)} %fusion.3), kind=kOutput, calls=%fused_computation.8 | convolution fusion | flops 3222798336 | bytes 17301504 | tf_op jit(solution)/shard_map/dot_general | solution.py:47
  148.9 6.6 %convolution_convert_fusion = bf16[2,512,16,384]{3,1,2,0:T(8,128)(2,1)} fusion(bf16[2,512,256,1]{2,1,3,0:T(8,128)(2,1)S(1)} %bitcast.65, bf16[256,16,384]{2,1,0:T(8,128)(2,1)S(1)} %bitcast.59), kind=kOutput, calls=%fused_computation | convolution fusion | flops 3227516928 | bytes 16252928 | tf_op jit(solution)/shard_map/cri,ifd->cfrd/dot_general | solution.py:55
  155.6 0.9 copy-done.2
  156.4 0.2 fusion.37
  156.6 11.1 %all_to_all.41 = f32[16,128,8]{1,2,0:T(8,128)} all-to-all(f32[16,128,8]{1,2,0:T(8,128)S(1)} %broadcast_in_dim.6), channel_id=1, replica_groups=mesh['dp'=2,'expert'=8,'ffn'=16] {'ffn'}, dimensions={0} | all-to-all | bytes 131072 | tf_op jit(solution)/shard_map/all_to_all | solution.py:9
  167.7 98.8 %reduce-scatter.2.cloned.1.call-done = bf16[512,384]{1,0:T(8,128)(2,1)} async-done(((bf16[16384,384]{1,0:T(8,128)(2,1)}), bf16[512,384]{1,0:T(8,128)(2,1)}) %reduce-scatter.2.cloned.1.call-update) | async-done | bytes 393232 | tf_op jit(solution)/shard_map/reduce_scatter | solution.py:59
  266.5 6.7 %all-to-all-start.2 = ((bf16[8,64,384]{2,1,0:T(8,128)(2,1)}), bf16[8,64,384]{2,1,0:T(8,128)(2,1)S(1)}, u32[]{:S(2)}, u32[]{:S(2)}) async-start(bf16[8,64,384]{2,1,0:T(8,128)(2,1)} %bitcast.66), calls=%async_computation.3 | async-start | bytes 786432 | tf_op jit(solution)/shard_map/all_to_all | solution.py:62
  273.2 0.5 convert_bitcast_fusion
  273.7 0.9 reduce_sum.81
  274.6 0.7 select_reduce_fusion.2
  275.3 0.6 copy-done.5
  275.9 0.6 subtract_multiply_fusion.2
  276.5 8.4 %all-to-all-done.2 = bf16[8,64,384]{2,1,0:T(8,128)(2,1)S(1)} async-done(((bf16[8,64,384]{2,1,0:T(8,128)(2,1)}), bf16[8,64,384]{2,1,0:T(8,128)(2,1)S(1)}, u32[]{:S(2)}, u32[]{:S(2)}) %all-to-all-start.2) | async-done | bytes 393248 | tf_op jit(solution)/shard_map/all_to_all | solution.py:62
  284.9 0.9 fusion.15
  285.8 1.7 multiply_reduce_fusion
  287.5 11.4 %all_to_all.42 = f32[16,1,128]{2,1,0:T(1,128)S(1)} all-to-all(f32[16,1,128]{2,1,0:T(1,128)S(1)} %broadcast_in_dim.7), channel_id=1, replica_groups=mesh['dp'=2,'expert'=8,'ffn'=16] {'ffn'}, dimensions={0} | all-to-all | bytes 16384 | tf_op jit(solution)/shard_map/all_to_all | solution.py:9
  299.0 0.7 fusion.31
  299.6 1.0 convolution_bitcast_fusion
  300.7 15.8 %all_to_all.43 = f32[16,384,8]{1,2,0:T(8,128)S(1)} all-to-all(f32[16,384,8]{1,2,0:T(8,128)S(1)} %broadcast_in_dim.8), channel_id=1, replica_groups=mesh['dp'=2,'expert'=8,'ffn'=16] {'dp','expert'}, dimensions={0} | all-to-all | bytes 393216 | tf_op jit(solution)/shard_map/all_to_all | solution.py:9
  316.5 0.6 reduce_sum.89
  (36 shorter events, 0.8 us)
Async XLA Ops:
  7.2 129.2 %copy-start = (bf16[1,6144,256]{2,1,0:T(8,128)(2,1)S(1)}, bf16[1,6144,256]{2,1,0:T(8,128)(2,1)}, u32[]{:S(2)}) copy-start(bf16[1,6144,256]{2,1,0:T(8,128)(2,1)} %param.11) | copy-start | bytes 9437188
  7.2 129.2 %all-gather.2.cloned.1.call-start = ((), (), s32[]{:S(2)}) async-start(), calls=%async_computation.6 | async-start | bytes 13369344 | tf_op jit(solution)/shard_map/all_gather | solution.py:45
  10.3 23.5 %copy-start.6 = (s32[128]{0:T(128)}, s32[128]{0:T(128)S(1)}, u32[]{:S(2)}) copy-start(s32[128]{0:T(128)S(1)} %get-tuple-element.20) | copy-start | bytes 1540
  10.3 23.5 %copy-start.7 = (s32[128]{0:T(128)}, s32[128]{0:T(128)S(1)}, u32[]{:S(2)}) copy-start(s32[128]{0:T(128)S(1)} %get-tuple-element.21) | copy-start | bytes 1540
  38.1 228.4 %reduce-scatter.2.cloned.1.call-start = ((), (), s32[]{:S(2)}) async-start(), calls=%async_computation.7 | async-start | bytes 12976128 | tf_op jit(solution)/shard_map/reduce_scatter | solution.py:59
  136.4 8.2 %copy-start.8 = (bf16[1024,6144]{1,0:T(8,128)(2,1)S(1)}, bf16[1024,6144]{1,0:T(8,128)(2,1)}, u32[]{:S(2)}) copy-start(bf16[1024,6144]{1,0:T(8,128)(2,1)} %all-gather.2.cloned.1.call-done) | copy-start | bytes 37748740
  136.4 9.1 %copy-start.9 = (bf16[1,6144,256]{2,1,0:T(8,128)(2,1)S(1)}, bf16[1,6144,256]{2,1,0:T(8,128)(2,1)}, u32[]{:S(2)}) copy-start(bf16[1,6144,256]{2,1,0:T(8,128)(2,1)} %param.12) | copy-start | bytes 9437188
  145.4 3.4 %copy-start.1 = (bf16[32,8,16,384]{3,2,1,0:T(8,128)(2,1)S(1)}, bf16[32,8,16,384]{3,2,1,0:T(8,128)(2,1)}, u32[]{:S(2)}) copy-start(bf16[32,8,16,384]{3,2,1,0:T(8,128)(2,1)} %copy.55) | copy-start | bytes 9437188
  155.5 0.9 copy-start.2
  155.5 0.9 copy-start.3
  155.5 117.7 %copy-start.10 = (s32[1,8]{1,0:T(1,128)S(1)}, s32[1,8]{1,0:T(1,128)}, u32[]{:S(2)}) copy-start(s32[1,8]{1,0:T(1,128)} %param.9) | copy-start | bytes 100
  155.5 118.2 %copy-start.4 = (s32[128,2]{0,1:T(2,128)S(1)}, s32[128,2]{0,1:T(2,128)}, u32[]{:S(2)}) copy-start(s32[128,2]{0,1:T(2,128)} %param.8) | copy-start | bytes 3076
  266.5 18.4 %all-to-all-start.2 = ((bf16[8,64,384]{2,1,0:T(8,128)(2,1)}), bf16[8,64,384]{2,1,0:T(8,128)(2,1)S(1)}, u32[]{:S(2)}, u32[]{:S(2)}) async-start(bf16[8,64,384]{2,1,0:T(8,128)(2,1)} %bitcast.66), calls=%async_computation.3 | async-start | bytes 786432 | tf_op jit(solution)/shard_map/all_to_all | solution.py:62
  275.3 0.6 copy-start.5
Sparse Core Ops, SparseCore 0:
  38.2 98.1 all-gather.1
  155.7 110.7 reduce-scatter.1
where the time goes:
time: 325 us; the launch traced here: 324 us
  waiting for transfers between devices  201 us (62%)
  blocking collectives  64.9 us (20%)
  matrix products  22.7 us (7%)
  between operations  14.2 us (4%)
  local copies, waits for them, and re-layouts  8.74 us (3%)
  starting transfers between devices  6.82 us (2%)
  other arithmetic  5.4 us (2%)
    reduce_scatter x1, waiting for transfers between devices, on_device(): lax.psum_scatter(terms.astype(jnp.bfloat16), ('dp', 'ffn'), scatter_dimen...  98.8 us
    all_gather x1, waiting for transfers between devices, on_device(): piece = lax.all_gather(slot_rows, 'ffn', axis=1, tiled=True)  94 us
    all_to_all x3, blocking collectives, from_everyone(): lax.all_to_all(jnp.broadcast_to(shard[None], (length, *shard.shape)), axi...  38.3 us
    all_to_all x1, blocking collectives, on_device(): lax.all_to_all(outgoing, 'expert', split_axis=0, concat_axis=0, tiled=True)  22.4 us
    all_to_all x1, waiting for transfers between devices, on_device(): lax.all_to_all(summed, 'expert', split_axis=0, concat_axis=0, tiled=True)  8.4 us
    unnamed x24, local copies, waits for them, and re-layouts  7.99 us
    dot_general x1, matrix products, on_device(): gate = jnp.dot(piece, gate_w, preferred_element_type=jnp.float32)  7.71 us
    all_to_all x1, starting transfers between devices, on_device(): lax.all_to_all(summed, 'expert', split_axis=0, concat_axis=0, tiled=True)  6.74 us
  transfers between devices with their start and end apart: 3, of which 3 were waited for; matrix products, arithmetic and copies ran while one was open for 2% of the time, Pallas kernels for 0%

commit v1 on v0

v1 whole, which is shorter than its diff:
```python
import functools

import jax
import jax.numpy as jnp
from jax import lax
from jax.experimental import pallas as pl
from jax.experimental.pallas import tpu as pltpu
from jax.sharding import PartitionSpec as P

MESH = pl.DeviceIdType.MESH
RING = 4
PLANE = RING * RING
HIGH = lax.Precision.HIGHEST


def kernel(
    nz, rows, cols, hid, tok_hbm, routes_hbm, keep_hbm, router_hbm, wg_hbm, wu_hbm, wd_hbm,
    full_hbm, pruned_hbm, resid_hbm, grad_hbm,
    tok, routes, keep, router, wg, wu, wd,
    X, lhs, T, Q, R0, RA1, RA2, RB1, RB2, out, ret,
    LD, LI, LG, stat, full_v, pruned_v, resid_v, grad_v,
    in_sem, out_sem, zin_sem, s1_sem, s1h_sem, s2_sem, s2h_sem, xx_sem, pp_sem,
    a1_sem, a2_sem, b1_sem, b2_sem, ret_sem, small_sem,
    send_ag, send_rs, send_x, send_p, send_z, send_r, send_small,
):
    f32, bf16 = jnp.float32, jnp.bfloat16
    d = lax.axis_index("dp")
    z = lax.axis_index("expert")
    f = lax.axis_index("ffn")
    y, x = f // RING, f % RING
    half = rows // 2
    toks = 2 * rows
    nq = 2 * nz
    me = d * nz + z

    m1, m2 = 1 + (RING - 1) * d, RING - (RING - 1) * d
    c1, c2 = x + d * (y - x), y + d * (x - y)

    def place(a1, a2):
        return ((c1 + a1) % RING) * m1 + ((c2 + a2) % RING) * m2

    up1, dn1, up2, dn2 = place(1, 0), place(3, 0), place(0, 1), place(0, 3)

    def send(src, dst, ssem, rsem, dev):
        pltpu.make_async_remote_copy(
            src_ref=src, dst_ref=dst, send_sem=ssem, recv_sem=rsem, device_id=dev, device_id_type=MESH
        ).start()

    def landed(ref, sem):
        pltpu.make_async_remote_copy(
            src_ref=ref, dst_ref=ref, send_sem=sem, recv_sem=sem, device_id={"ffn": up1}, device_id_type=MESH
        ).wait_recv()

    def sent(ref, sem):
        pltpu.make_async_remote_copy(
            src_ref=ref, dst_ref=ref, send_sem=sem, recv_sem=sem, device_id={"ffn": up1}, device_id_type=MESH
        ).wait_send()

    def plane(p):
        return {"ffn": p}

    barrier = pltpu.get_barrier_semaphore()
    for j in range(1, PLANE):
        pl.semaphore_signal(barrier, inc=1, device_id={"ffn": (f + j) % PLANE}, device_id_type=MESH)
    for j in range(1, nq):
        q = (me + j) % nq
        pl.semaphore_signal(barrier, inc=1, device_id={"dp": q // nz, "expert": q % nz}, device_id_type=MESH)

    loads = [
        pltpu.make_async_copy(routes_hbm, routes, in_sem.at[0]),
        pltpu.make_async_copy(tok_hbm, tok, in_sem.at[1]),
        pltpu.make_async_copy(keep_hbm, keep, in_sem.at[2]),
        pltpu.make_async_copy(router_hbm, router, in_sem.at[3]),
        pltpu.make_async_copy(wg_hbm.at[0], wg, in_sem.at[4]),
        pltpu.make_async_copy(wu_hbm.at[0], wu, in_sem.at[5]),
        pltpu.make_async_copy(wd_hbm.at[0], wd, in_sem.at[6]),
    ]
    for load in loads:
        load.start()

    loads[0].wait()
    r0 = routes[0:1, :]
    r1 = routes[1:2, :]
    expert_rows = lax.broadcasted_iota(jnp.int32, (nz, toks), 0)
    oh0 = (expert_rows == r0).astype(f32)
    oh1 = (expert_rows == r1).astype(f32)
    earlier = (
        lax.broadcasted_iota(jnp.int32, (toks, toks), 0) < lax.broadcasted_iota(jnp.int32, (toks, toks), 1)
    ).astype(bf16)
    before = jnp.dot((oh0 + oh1).astype(bf16), earlier, preferred_element_type=f32)
    pos0 = r0.astype(f32) * rows + jnp.sum(before * oh0, axis=0, keepdims=True)
    pos1 = r1.astype(f32) * rows + jnp.sum(before * oh1, axis=0, keepdims=True)

    loads[1].wait()
    slot = lax.broadcasted_iota(jnp.int32, (rows, toks), 0)
    for k in range(nz):
        e = (z + nz - k) % nz
        at = (slot + e * rows).astype(f32)
        pick = jnp.logical_or(at == pos0, at == pos1).astype(f32).astype(bf16)
        picked = jnp.dot(pick, tok[...], preferred_element_type=f32).astype(bf16)
        if k == 0:
            X[0, 0, f] = picked
        else:
            out[k] = picked
    pl.semaphore_wait(barrier, PLANE - 1 + nq - 1)
    for k in range(1, nz):
        send(out.at[k], X.at[0, k, f], send_z.at[k], zin_sem.at[k], {"expert": (z + nz - k) % nz})

    def ag_a(k):
        @pl.when(k > 0)
        def _():
            landed(X.at[0, k, f], zin_sem.at[k])

        own = X.at[0, k, f]
        send(own, own, send_ag.at[k], s1_sem.at[k, 0], plane(up1))
        send(own, own, send_ag.at[k], s1_sem.at[k, 1], plane(dn1))
        send(own, own, send_ag.at[k], s2_sem.at[k, 0, 0], plane(up2))
        send(own, own, send_ag.at[k], s2_sem.at[k, 1, 0], plane(dn2))

    lo, hi = pl.ds(0, half), pl.ds(half, half)

    def across(k, p, r):
        ref = X.at[0, k, p]
        send(ref, ref, send_ag.at[k], s2_sem.at[k, 0, r], plane(up2))
        send(ref, ref, send_ag.at[k], s2_sem.at[k, 1, r], plane(dn2))

    def ag_b(k):
        landed(X.at[0, k, dn1], s1_sem.at[k, 0])
        send(X.at[0, k, dn1, lo], X.at[0, k, dn1, lo], send_ag.at[k], s1h_sem.at[k, 0], plane(up1))
        across(k, dn1, 1)
        landed(X.at[0, k, up1], s1_sem.at[k, 1])
        send(X.at[0, k, up1, hi], X.at[0, k, up1, hi], send_ag.at[k], s1h_sem.at[k, 1], plane(dn1))
        across(k, up1, 2)

    def ag_c(k):
        op1 = place(2, 0)
        landed(X.at[0, k, op1, lo], s1h_sem.at[k, 0])
        landed(X.at[0, k, op1, hi], s1h_sem.at[k, 1])
        across(k, op1, 3)

    turns = (0, 3, 1, 2)

    def ag_d(k):
        for r, a1 in enumerate(turns):
            p = place(a1, 3)
            landed(X.at[0, k, p], s2_sem.at[k, 0, r])
            send(X.at[0, k, p, lo], X.at[0, k, p, lo], send_ag.at[k], s2h_sem.at[k, 0, r], plane(up2))
            p = place(a1, 1)
            landed(X.at[0, k, p], s2_sem.at[k, 1, r])
            send(X.at[0, k, p, hi], X.at[0, k, p, hi], send_ag.at[k], s2h_sem.at[k, 1, r], plane(dn2))

    def ag_e(k):
        for r, a1 in enumerate(turns):
            p = place(a1, 2)
            landed(X.at[0, k, p, lo], s2h_sem.at[k, 0, r])
            landed(X.at[0, k, p, hi], s2h_sem.at[k, 1, r])
        send(X.at[0, k], X.at[1, k], send_x.at[k], xx_sem.at[k], {"dp": 1 - d})

    def work(k):
        landed(X.at[1, k], xx_sem.at[k])
        for c in range(2):
            for s in range(PLANE):
                lhs[c * rows:(c + 1) * rows, s * cols:(s + 1) * cols] = X[c, k, s]
        gate = jnp.dot(lhs[...], wg[...], preferred_element_type=f32)
        up = jnp.dot(lhs[...], wu[...], preferred_element_type=f32)
        hidden = (gate / (1.0 + jnp.exp(-gate)) * up).astype(bf16)
        for s in range(0, PLANE, 2):
            part = jnp.dot(hidden, wd[:, s * cols:(s + 2) * cols], preferred_element_type=f32).astype(bf16)
            for t in range(2):
                T[k, s + t] = part[0:rows, t * cols:(t + 1) * cols]
                Q[k, s + t] = part[rows:, t * cols:(t + 1) * cols]
        send(Q.at[k], R0.at[k], send_p.at[k], pp_sem.at[k], {"dp": 1 - d})

    def rs_1(k):
        landed(R0.at[k], pp_sem.at[k])
        for a2 in (2, 1, 3, 0):
            for a1 in range(RING):
                p = place(a1, a2)
                T[k, p] = T[k, p] + R0[k, p]
            if a2 == 2:
                for a1 in range(RING):
                    p = place(a1, a2)
                    send(T.at[k, p, lo], RA1.at[k, 0, a1], send_rs.at[k], a1_sem.at[k, 0], plane(up2))
                    send(T.at[k, p, hi], RA1.at[k, 1, a1], send_rs.at[k], a1_sem.at[k, 1], plane(dn2))

    def rs_2(k):
        landed(RA1.at[k, 0], a1_sem.at[k, 0])
        for a1 in range(RING):
            p = place(a1, 1)
            T[k, p, lo] = T[k, p, lo] + RA1[k, 0, a1]
        for a1 in range(RING):
            send(T.at[k, place(a1, 1)], RA2.at[k, 0, a1], send_rs.at[k], a2_sem.at[k, 0], plane(up2))
        landed(RA1.at[k, 1], a1_sem.at[k, 1])
        for a1 in range(RING):
            p = place(a1, 3)
            T[k, p, hi] = T[k, p, hi] + RA1[k, 1, a1]
        for a1 in range(RING):
            send(T.at[k, place(a1, 3)], RA2.at[k, 1, a1], send_rs.at[k], a2_sem.at[k, 1], plane(dn2))

    def total(own, one, two):
        return (own.astype(f32) + one.astype(f32) + two.astype(f32)).astype(bf16)

    def rs_3(k):
        landed(RA2.at[k, 0], a2_sem.at[k, 0])
        landed(RA2.at[k, 1], a2_sem.at[k, 1])
        for a1 in (2, 1, 3, 0):
            p = place(a1, 0)
            T[k, p] = total(T[k, p], RA2[k, 0, a1], RA2[k, 1, a1])
            if a1 == 2:
                send(T.at[k, p, lo], RB1.at[k, 0], send_rs.at[k], b1_sem.at[k, 0], plane(up1))
                send(T.at[k, p, hi], RB1.at[k, 1], send_rs.at[k], b1_sem.at[k, 1], plane(dn1))

    def rs_4(k):
        landed(RB1.at[k, 0], b1_sem.at[k, 0])
        T[k, up1, lo] = T[k, up1, lo] + RB1[k, 0]
        send(T.at[k, up1], RB2.at[k, 0], send_rs.at[k], b2_sem.at[k, 0], plane(up1))
        landed(RB1.at[k, 1], b1_sem.at[k, 1])
        T[k, dn1, hi] = T[k, dn1, hi] + RB1[k, 1]
        send(T.at[k, dn1], RB2.at[k, 1], send_rs.at[k], b2_sem.at[k, 1], plane(dn1))

    def rs_5(k):
        landed(RB2.at[k, 0], b2_sem.at[k, 0])
        landed(RB2.at[k, 1], b2_sem.at[k, 1])
        summed = total(T[k, f], RB2[k, 0], RB2[k, 1])

        @pl.when(k == 0)
        def _():
            ret[z] = summed

        @pl.when(k > 0)
        def _():
            T[k, f] = summed
            send(T.at[k, f], ret.at[z], send_r.at[k], ret_sem.at[k], {"expert": (z + k) % nz})

    def logits_out():
        loads[3].wait()
        local = lax.dot_general(
            router[...], tok[...].astype(f32), (((1,), (1,)), ((), ())), precision=HIGH, preferred_element_type=f32
        )
        part = jnp.sum(local * (oh0 - oh1), axis=0, keepdims=True)
        LD[f] = jnp.broadcast_to(part, (8, toks))
        for j in range(1, PLANE):
            send(LD.at[f], LD.at[f], send_small.at[0], small_sem.at[0], plane((f + j) % PLANE))

    def when(k, stage):
        @pl.when(jnp.logical_and(k >= 0, k < nz))
        def _():
            stage(k)

    @pl.loop(0, nz + 9)
    def _(i):
        when(i, ag_a)
        when(i - 1, ag_b)
        when(i - 2, ag_c)
        when(i - 2, ag_d)
        when(i - 3, ag_e)

        @pl.when(i == 1)
        def _():
            logits_out()

        @pl.when(i == 4)
        def _():
            loads[4].wait()
            loads[5].wait()
            loads[6].wait()

        when(i - 4, work)
        when(i - 5, rs_1)
        when(i - 6, rs_2)
        when(i - 7, rs_3)
        when(i - 8, rs_4)
        when(i - 9, rs_5)

    loads[2].wait()
    landed(LD.at[pl.ds(0, PLANE - 1)], small_sem.at[0])
    diff = jnp.sum(LD[...], axis=0)[0:1]
    wide = jnp.broadcast_to(keep[...].astype(f32), (nz, nz))
    diagonal = lax.broadcasted_iota(jnp.int32, (nz, nz), 0) == lax.broadcasted_iota(jnp.int32, (nz, nz), 1)
    keep_column = jnp.sum(jnp.where(diagonal, wide, 0.0), axis=1, keepdims=True)
    keep0 = jnp.sum(keep_column * oh0, axis=0, keepdims=True)
    keep1 = jnp.sum(keep_column * oh1, axis=0, keepdims=True)
    stat[...] = jnp.zeros_like(stat)
    for j, row in enumerate((pos0, pos1, diff, keep0, keep1)):
        stat[j:j + 1, :] = row
    columns = jnp.transpose(stat[...])
    p0, p1, dc, k0, k1 = (columns[:, j:j + 1] for j in range(5))
    slots = lax.broadcasted_iota(jnp.int32, (toks, nz * rows), 1).astype(f32)
    pick0 = (slots == p0).astype(f32).astype(bf16)
    pick1 = (slots == p1).astype(f32).astype(bf16)
    share, other = 1.0 / (1.0 + jnp.exp(-dc)), 1.0 / (1.0 + jnp.exp(dc))
    pruned0 = k0 * (k1 * share + 1.0 - k1)
    pruned1 = k1 * (k0 * other + 1.0 - k0)

    for k in range(1, nz):
        landed(ret.at[k], ret_sem.at[k])
    returned = ret[...].reshape(nz * rows, cols)
    first = jnp.dot(pick0, returned, preferred_element_type=f32)
    second = jnp.dot(pick1, returned, preferred_element_type=f32)
    full32 = share * first + other * second
    pruned32 = pruned0 * first + pruned1 * second
    residual = full32 - pruned32
    inner_part = jnp.sum(residual * (first - second), axis=1, keepdims=True)
    LI[f] = jnp.transpose(jnp.broadcast_to(inner_part, (toks, 128)))[0:8]
    for j in range(1, PLANE):
        send(LI.at[f], LI.at[f], send_small.at[1], small_sem.at[1], plane((f + j) % PLANE))
    full_v[...] = full32.astype(bf16)
    pruned_v[...] = pruned32.astype(bf16)
    resid_v[...] = residual
    stores = [
        pltpu.make_async_copy(full_v, full_hbm, out_sem.at[0]),
        pltpu.make_async_copy(pruned_v, pruned_hbm, out_sem.at[1]),
        pltpu.make_async_copy(resid_v, resid_hbm, out_sem.at[2]),
    ]
    for store in stores:
        store.start()
    share_row = 1.0 / (1.0 + jnp.exp(-diff))
    rate = share_row * (1.0 - share_row) * (1.0 - keep0 * keep1)
    landed(LI.at[pl.ds(0, PLANE - 1)], small_sem.at[1])
    inner = jnp.sum(LI[...], axis=0)[0:1]
    slope = rate * inner
    LG[me] = jnp.dot(
        (oh0 - oh1) * slope, tok[...].astype(f32), precision=HIGH, preferred_element_type=f32
    )
    for j in range(1, nq):
        q = (me + j) % nq
        send(LG.at[me], LG.at[me], send_small.at[2], small_sem.at[2], {"dp": q // nz, "expert": q % nz})
    landed(LG.at[pl.ds(0, nq - 1)], small_sem.at[2])
    grad_v[...] = jnp.sum(LG[...], axis=0)
    last = pltpu.make_async_copy(grad_v, grad_hbm, out_sem.at[3])
    last.start()

    sent(LD.at[pl.ds(0, PLANE - 1)], send_small.at[0])
    sent(LI.at[pl.ds(0, PLANE - 1)], send_small.at[1])
    sent(LG.at[pl.ds(0, nq - 1)], send_small.at[2])

    @pl.loop(0, nz)
    def _(k):
        sent(X.at[0, k, pl.ds(0, 15)], send_ag.at[k])
        sent(T.at[k, pl.ds(0, 15)], send_rs.at[k])
        sent(X.at[0, k], send_x.at[k])
        sent(Q.at[k], send_p.at[k])

    for k in range(1, nz):
        sent(out.at[k], send_z.at[k])
        sent(T.at[k, f], send_r.at[k])
    for store in stores:
        store.wait()
    last.wait()


def layer(nz, tokens, routes, keep, router, w_gate, w_up, w_down):
    toks, cols = tokens.shape
    rows = toks // 2
    depth, hid = w_gate.shape[1:]
    bf16, f32 = jnp.bfloat16, jnp.float32
    vmem, dma = pltpu.VMEM, pltpu.SemaphoreType.DMA
    shard = (rows, cols)
    piece = (rows // 2, cols)
    nq = 2 * nz
    anywhere = pl.BlockSpec(memory_space=pl.ANY)
    out = pl.pallas_call(
        functools.partial(kernel, nz, rows, cols, hid),
        out_shape=(
            jax.ShapeDtypeStruct((toks, cols), bf16),
            jax.ShapeDtypeStruct((toks, cols), bf16),
            jax.ShapeDtypeStruct((toks, cols), f32),
            jax.ShapeDtypeStruct((nz, cols), f32),
        ),
        in_specs=[anywhere] * 7,
        out_specs=(anywhere,) * 4,
        scratch_shapes=[
            vmem((toks, cols), bf16), vmem((2, toks), jnp.int32), vmem((1, nz), jnp.int32), vmem((nz, cols), f32),
            vmem((depth, hid), bf16), vmem((depth, hid), bf16), vmem((hid, depth), bf16),
            vmem((2, nz, PLANE, *shard), bf16), vmem((toks, depth), bf16),
            vmem((nz, PLANE, *shard), bf16), vmem((nz, PLANE, *shard), bf16), vmem((nz, PLANE, *shard), bf16),
            vmem((nz, 2, RING, *piece), bf16), vmem((nz, 2, RING, *shard), bf16),
            vmem((nz, 2, *piece), bf16), vmem((nz, 2, *shard), bf16),
            vmem((nz, *shard), bf16), vmem((nz, *shard), bf16),
            vmem((PLANE, 8, toks), f32), vmem((PLANE, 8, toks), f32), vmem((nq, nz, cols), f32),
            vmem((128, toks), f32),
            vmem((toks, cols), bf16), vmem((toks, cols), bf16), vmem((toks, cols), f32), vmem((nz, cols), f32),
            dma((7,)), dma((4,)), dma((nz,)), dma((nz, 2)), dma((nz, 2)), dma((nz, 2, RING)), dma((nz, 2, RING)),
            dma((nz,)), dma((nz,)),
            dma((nz, 2)), dma((nz, 2)), dma((nz, 2)), dma((nz, 2)), dma((nz,)), dma((3,)),
            dma((nz,)), dma((nz,)), dma((nz,)), dma((nz,)), dma((nz,)), dma((nz,)), dma((3,)),
        ],
        compiler_params=pltpu.CompilerParams(
            collective_id=0, has_side_effects=True, vmem_limit_bytes=60 * 1024 * 1024
        ),
        name="layer",
    )(tokens, routes.T, keep, router.T, w_gate, w_up, w_down)
    return out[0], out[1], out[2], out[3].T


def solution(mesh):
    return jax.shard_map(
        functools.partial(layer, mesh.shape["expert"]),
        mesh=mesh,
        in_specs=(
            P(("dp", "expert"), "ffn"),
            P(("dp", "expert"), None),
            P(("dp", "expert"), None),
            P("ffn", None),
            P("expert", None, ("dp", "ffn")),
            P("expert", None, ("dp", "ffn")),
            P("expert", ("dp", "ffn"), None),
        ),
        out_specs=(
            P(("dp", "expert"), "ffn"),
            P(("dp", "expert"), "ffn"),
            P(("dp", "expert"), "ffn"),
            P("ffn", None),
        ),
        check_vma=False,
    )
```

time: 325 us -> 137 us (0.42)
  waiting for transfers between devices: 201 us -> 0 us
  Pallas kernels: 0 us -> 131 us
  blocking collectives: 64.9 us -> 0 us
  matrix products: 22.7 us -> 0 us
  between operations: 14.2 us -> 0.64 us
  starting transfers between devices: 6.82 us -> 0 us
  other arithmetic: 5.4 us -> 0 us
    pallas_call x0 -> x1, Pallas kernels: none -> 131 us  [layer(): pl.pallas_call(functools.partial(kernel, nz, rows, cols, hid), out_shape=...]
    reduce_scatter x1 -> x0, waiting for transfers between devices: 98.8 us -> none  [on_device(): lax.psum_scatter(terms.astype(jnp.bfloat16), ('dp', 'ffn'), scatter_dimen...]
    all_gather x1 -> x0, waiting for transfers between devices: 94 us -> none  [on_device(): piece = lax.all_gather(slot_rows, 'ffn', axis=1, tiled=True)]
    all_to_all x4 -> x0, blocking collectives: 60.7 us -> none  [the longest x3 38.3 us: from_everyone(): lax.all_to_all(jnp.broadcast_to(shard[None], (length, *shard.shape)), axi...]
    dot_general x8 -> x0, matrix products: 22.7 us -> none  [the longest x1 7.71 us: on_device(): gate = jnp.dot(piece, gate_w, preferred_element_type=jnp.float32)]
    all_to_all x1 -> x0, waiting for transfers between devices: 8.4 us -> none  [on_device(): lax.all_to_all(summed, 'expert', split_axis=0, concat_axis=0, tiled=True)]
    all_to_all x1 -> x0, starting transfers between devices: 6.74 us -> none  [on_device(): lax.all_to_all(summed, 'expert', split_axis=0, concat_axis=0, tiled=True)]
    all_gather x1 -> x0, blocking collectives: 4.18 us -> none  [on_device(): slot_rows = lax.all_gather(arrived, 'dp', axis=0, tiled=True)]
  transfers between devices with their start and end apart: 3 -> 0, of which waited for: 3 -> 0; matrix products, arithmetic and copies ran while one was open for 2% -> 0% of each run, Pallas kernels for 0% -> 0%
where the time goes in v1:
time: 137 us
  Pallas kernels  131 us (96%)
  local copies, waits for them, and re-layouts  6.01 us (4%)
    pallas_call x1, Pallas kernels, layer(): pl.pallas_call(functools.partial(kernel, nz, rows, cols, hid), out_shape=...  131 us
    unnamed x4, local copies, waits for them, and re-layouts  6.01 us

profile of v1, /device:TPU:1, one launch (start us, length us, event | category | flops | bytes accessed | tf_op | source)
XLA Modules:
  0.0 137.2 jit_solution(3814125040126719216)
XLA Ops:
  0.6 130.5 %layer.1 = (bf16[128,384]{1,0:T(8,128)(2,1)}, bf16[128,384]{1,0:T(8,128)(2,1)}, f32[128,384]{1,0:T(8,128)}, f32[8,384]{1,0:T(8,128)}) custom-call(bf16[128,384]{1,0:T(8,128)(2,1)} %tok_hbm.1, s32[2,128]{1,0:T(2,128)} %bitcast.5, s32[1,8]{1,0:T(1,128)} %keep_hbm.1, f32[8,384]{1,0:T(8,128)} %bitcast.4, bf16[1,6144,256]{2,1,0:T(8,128)(2,1)} %wg_hbm.1, ...), custom_call_target="tpu_custom_call" | custom-call | tf_op jit(solution)/shard_map/layer/pallas_call | solution.py:362
  131.2 1.5 %copy.15 = bf16[128,384]{1,0:T(8,128)(2,1)} copy(bf16[128,384]{1,0:T(8,128)(2,1)} %get-tuple-element.16) | data formatting | bytes 196608
  132.7 1.5 %copy.16 = bf16[128,384]{1,0:T(8,128)(2,1)} copy(bf16[128,384]{1,0:T(8,128)(2,1)} %get-tuple-element.17) | data formatting | bytes 196608
  134.3 1.6 %copy.17 = f32[128,384]{1,0:T(8,128)} copy(f32[128,384]{1,0:T(8,128)} %get-tuple-element.18) | data formatting | bytes 393216
  135.9 1.3 copy.18

commit v2 on v1

--- a/solution.py
+++ b/solution.py
@@ -11,15 +11,16 @@
 RING = 4
 PLANE = RING * RING
 HIGH = lax.Precision.HIGHEST
+LAG = 6
 
 
 def kernel(
     nz, rows, cols, hid, tok_hbm, routes_hbm, keep_hbm, router_hbm, wg_hbm, wu_hbm, wd_hbm,
-    full_hbm, pruned_hbm, resid_hbm, grad_hbm,
+    full_v, pruned_v, resid_v, grad_v,
     tok, routes, keep, router, wg, wu, wd,
     X, lhs, T, Q, R0, RA1, RA2, RB1, RB2, out, ret,
-    LD, LI, LG, stat, full_v, pruned_v, resid_v, grad_v,
-    in_sem, out_sem, zin_sem, s1_sem, s1h_sem, s2_sem, s2h_sem, xx_sem, pp_sem,
+    LD, LI, LG, stat,
+    in_sem, zin_sem, s1_sem, s1h_sem, s2_sem, s2h_sem, xx_sem, pp_sem,
     a1_sem, a2_sem, b1_sem, b2_sem, ret_sem, small_sem,
     send_ag, send_rs, send_x, send_p, send_z, send_r, send_small,
 ):
@@ -140,14 +141,18 @@
 
     turns = (0, 3, 1, 2)
 
-    def ag_d(k):
-        for r, a1 in enumerate(turns):
+    def ag_d(k, which=(0, 1, 2)):
+        for r in which:
+            a1 = turns[r]
             p = place(a1, 3)
             landed(X.at[0, k, p], s2_sem.at[k, 0, r])
             send(X.at[0, k, p, lo], X.at[0, k, p, lo], send_ag.at[k], s2h_sem.at[k, 0, r], plane(up2))
             p = place(a1, 1)
             landed(X.at[0, k, p], s2_sem.at[k, 1, r])
             send(X.at[0, k, p, hi], X.at[0, k, p, hi], send_ag.at[k], s2h_sem.at[k, 1, r], plane(dn2))
+
+    def ag_d3(k):
+        ag_d(k, (3,))
 
     def ag_e(k):
         for r, a1 in enumerate(turns):
@@ -171,42 +176,49 @@
                 Q[k, s + t] = part[rows:, t * cols:(t + 1) * cols]
         send(Q.at[k], R0.at[k], send_p.at[k], pp_sem.at[k], {"dp": 1 - d})
 
+    order = (2, 1, 3, 0)
+
     def rs_1(k):
         landed(R0.at[k], pp_sem.at[k])
+
+        def across_1(a1):
+            p = place(a1, 2)
+            send(T.at[k, p, lo], RA1.at[k, 0, a1], send_rs.at[k], a1_sem.at[k, 0, a1], plane(up2))
+            send(T.at[k, p, hi], RA1.at[k, 1, a1], send_rs.at[k], a1_sem.at[k, 1, a1], plane(dn2))
+
+        held = None
         for a2 in (2, 1, 3, 0):
-            for a1 in range(RING):
+            for a1 in order:
                 p = place(a1, a2)
                 T[k, p] = T[k, p] + R0[k, p]
-            if a2 == 2:
-                for a1 in range(RING):
-                    p = place(a1, a2)
-                    send(T.at[k, p, lo], RA1.at[k, 0, a1], send_rs.at[k], a1_sem.at[k, 0], plane(up2))
-                    send(T.at[k, p, hi], RA1.at[k, 1, a1], send_rs.at[k], a1_sem.at[k, 1], plane(dn2))
+                if held is not None:
+                    across_1(held)
+                held = a1 if a2 == 2 else None
 
     def rs_2(k):
-        landed(RA1.at[k, 0], a1_sem.at[k, 0])
-        for a1 in range(RING):
-            p = place(a1, 1)
+        held = None
+        for a1 in order:
+            p, q = place(a1, 1), place(a1, 3)
+            landed(RA1.at[k, 0, a1], a1_sem.at[k, 0, a1])
             T[k, p, lo] = T[k, p, lo] + RA1[k, 0, a1]
-        for a1 in range(RING):
-            send(T.at[k, place(a1, 1)], RA2.at[k, 0, a1], send_rs.at[k], a2_sem.at[k, 0], plane(up2))
-        landed(RA1.at[k, 1], a1_sem.at[k, 1])
-        for a1 in range(RING):
-            p = place(a1, 3)
-            T[k, p, hi] = T[k, p, hi] + RA1[k, 1, a1]
-        for a1 in range(RING):
-            send(T.at[k, place(a1, 3)], RA2.at[k, 1, a1], send_rs.at[k], a2_sem.at[k, 1], plane(dn2))
+            if held is not None:
+                send(T.at[k, place(held, 3)], RA2.at[k, 1, held], send_rs.at[k], a2_sem.at[k, 1, held], plane(dn2))
+            landed(RA1.at[k, 1, a1], a1_sem.at[k, 1, a1])
+            T[k, q, hi] = T[k, q, hi] + RA1[k, 1, a1]
+            send(T.at[k, p], RA2.at[k, 0, a1], send_rs.at[k], a2_sem.at[k, 0, a1], plane(up2))
+            held = a1
+        send(T.at[k, place(held, 3)], RA2.at[k, 1, held], send_rs.at[k], a2_sem.at[k, 1, held], plane(dn2))
 
     def total(own, one, two):
         return (own.astype(f32) + one.astype(f32) + two.astype(f32)).astype(bf16)
 
     def rs_3(k):
-        landed(RA2.at[k, 0], a2_sem.at[k, 0])
-        landed(RA2.at[k, 1], a2_sem.at[k, 1])
-        for a1 in (2, 1, 3, 0):
+        for a1 in order:
+            landed(RA2.at[k, 0, a1], a2_sem.at[k, 0, a1])
+            landed(RA2.at[k, 1, a1], a2_sem.at[k, 1, a1])
             p = place(a1, 0)
             T[k, p] = total(T[k, p], RA2[k, 0, a1], RA2[k, 1, a1])
-            if a1 == 2:
+            if a1 == order[0]:
                 send(T.at[k, p, lo], RB1.at[k, 0], send_rs.at[k], b1_sem.at[k, 0], plane(up1))
                 send(T.at[k, p, hi], RB1.at[k, 1], send_rs.at[k], b1_sem.at[k, 1], plane(dn1))
 
@@ -247,30 +259,32 @@
         def _():
             stage(k)
 
-    @pl.loop(0, nz + 9)
+    @pl.loop(0, nz + LAG + 4)
     def _(i):
-        when(i, ag_a)
         when(i - 1, ag_b)
         when(i - 2, ag_c)
         when(i - 2, ag_d)
-        when(i - 3, ag_e)
+        when(i - 3, ag_d3)
+        when(i - 4, ag_e)
+        when(2 * i - 1, ag_a)
+        when(2 * i, ag_a)
 
         @pl.when(i == 1)
         def _():
             logits_out()
 
-        @pl.when(i == 4)
+        @pl.when(i == 5)
         def _():
             loads[4].wait()
             loads[5].wait()
             loads[6].wait()
 
-        when(i - 4, work)
-        when(i - 5, rs_1)
-        when(i - 6, rs_2)
-        when(i - 7, rs_3)
-        when(i - 8, rs_4)
-        when(i - 9, rs_5)
+        when(i - 5, work)
+        when(i - LAG, rs_1)
+        when(i - LAG - 1, rs_2)
+        when(i - LAG - 2, rs_3)
+        when(i - LAG - 3, rs_4)
+        when(i - LAG - 4, rs_5)
 
     loads[2].wait()
     landed(LD.at[pl.ds(0, PLANE - 1)], small_sem.at[0])
@@ -307,33 +321,9 @@
     full_v[...] = full32.astype(bf16)
     pruned_v[...] = pruned32.astype(bf16)
     resid_v[...] = residual
-    stores = [
-        pltpu.make_async_copy(full_v, full_hbm, out_sem.at[0]),
-        pltpu.make_async_copy(pruned_v, pruned_hbm, out_sem.at[1]),
-        pltpu.make_async_copy(resid_v, resid_hbm, out_sem.at[2]),
-    ]
-    for store in stores:
-        store.start()
     share_row = 1.0 / (1.0 + jnp.exp(-diff))
     rate = share_row * (1.0 - share_row) * (1.0 - keep0 * keep1)
-    landed(LI.at[pl.ds(0, PLANE - 1)], small_sem.at[1])
-    inner = jnp.sum(LI[...], axis=0)[0:1]
-    slope = rate * inner
-    LG[me] = jnp.dot(
-        (oh0 - oh1) * slope, tok[...].astype(f32), precision=HIGH, preferred_element_type=f32
-    )
-    for j in range(1, nq):
-        q = (me + j) % nq
-        send(LG.at[me], LG.at[me], send_small.at[2], small_sem.at[2], {"dp": q // nz, "expert": q % nz})
-    landed(LG.at[pl.ds(0, nq - 1)], small_sem.at[2])
-    grad_v[...] = jnp.sum(LG[...], axis=0)
-    last = pltpu.make_async_copy(grad_v, grad_hbm, out_sem.at[3])
-    last.start()
-
     sent(LD.at[pl.ds(0, PLANE - 1)], send_small.at[0])
-    sent(LI.at[pl.ds(0, PLANE - 1)], send_small.at[1])
-    sent(LG.at[pl.ds(0, nq - 1)], send_small.at[2])
-
     @pl.loop(0, nz)
     def _(k):
         sent(X.at[0, k, pl.ds(0, 15)], send_ag.at[k])
@@ -344,9 +334,28 @@
     for k in range(1, nz):
         sent(out.at[k], send_z.at[k])
         sent(T.at[k, f], send_r.at[k])
-    for store in stores:
-        store.wait()
-    last.wait()
+    landed(LI.at[pl.ds(0, PLANE - 1)], small_sem.at[1])
+    inner = jnp.sum(LI[...], axis=0)[0:1]
+    slope = rate * inner
+    LG[me] = jnp.dot(
+        (oh0 - oh1) * slope, tok[...].astype(f32), precision=HIGH, preferred_element_type=f32
+    ).astype(bf16)
+    for j in range(1, nq):
+        q = (me + j) % nq
+        send(LG.at[me], LG.at[me], send_small.at[2], small_sem.at[2], {"dp": q // nz, "expert": q % nz})
+    landed(LG.at[pl.ds(0, nq - 1)], small_sem.at[2])
+    grad_v[...] = jnp.sum(LG[...].astype(f32), axis=0)
+    sent(LI.at[pl.ds(0, PLANE - 1)], send_small.at[1])
+    sent(LG.at[pl.ds(0, nq - 1)], send_small.at[2])
+
+
+def store(*refs):
+    sem = refs[8]
+    copies = [pltpu.make_async_copy(refs[j], refs[4 + j], sem.at[j]) for j in range(4)]
+    for copy in copies:
+        copy.start()
+    for copy in copies:
+        copy.wait()
 
 
 def layer(nz, tokens, routes, keep, router, w_gate, w_up, w_down):
@@ -359,16 +368,12 @@
     piece = (rows // 2, cols)
     nq = 2 * nz
     anywhere = pl.BlockSpec(memory_space=pl.ANY)
-    out = pl.pallas_call(
+    shapes = (((toks, cols), bf16), ((toks, cols), bf16), ((toks, cols), f32), ((nz, cols), f32))
+    held = pl.pallas_call(
         functools.partial(kernel, nz, rows, cols, hid),
-        out_shape=(
-            jax.ShapeDtypeStruct((toks, cols), bf16),
-            jax.ShapeDtypeStruct((toks, cols), bf16),
-            jax.ShapeDtypeStruct((toks, cols), f32),
-            jax.ShapeDtypeStruct((nz, cols), f32),
-        ),
+        out_shape=tuple(vmem(*s) for s in shapes),
         in_specs=[anywhere] * 7,
-        out_specs=(anywhere,) * 4,
+        out_specs=(pl.BlockSpec(memory_space=vmem),) * 4,
         scratch_shapes=[
             vmem((toks, cols), bf16), vmem((2, toks), jnp.int32), vmem((1, nz), jnp.int32), vmem((nz, cols), f32),
             vmem((depth, hid), bf16), vmem((depth, hid), bf16), vmem((hid, depth), bf16),
@@ -377,12 +382,11 @@
             vmem((nz, 2, RING, *piece), bf16), vmem((nz, 2, RING, *shard), bf16),
             vmem((nz, 2, *piece), bf16), vmem((nz, 2, *shard), bf16),
             vmem((nz, *shard), bf16), vmem((nz, *shard), bf16),
-            vmem((PLANE, 8, toks), f32), vmem((PLANE, 8, toks), f32), vmem((nq, nz, cols), f32),
+            vmem((PLANE, 8, toks), f32), vmem((PLANE, 8, toks), f32), vmem((nq, nz, cols), bf16),
             vmem((128, toks), f32),
-            vmem((toks, cols), bf16), vmem((toks, cols), bf16), vmem((toks, cols), f32), vmem((nz, cols), f32),
-            dma((7,)), dma((4,)), dma((nz,)), dma((nz, 2)), dma((nz, 2)), dma((nz, 2, RING)), dma((nz, 2, RING)),
+            dma((7,)), dma((nz,)), dma((nz, 2)), dma((nz, 2)), dma((nz, 2, RING)), dma((nz, 2, RING)),
             dma((nz,)), dma((nz,)),
-            dma((nz, 2)), dma((nz, 2)), dma((nz, 2)), dma((nz, 2)), dma((nz,)), dma((3,)),
+            dma((nz, 2, RING)), dma((nz, 2, RING)), dma((nz, 2)), dma((nz, 2)), dma((nz,)), dma((3,)),
             dma((nz,)), dma((nz,)), dma((nz,)), dma((nz,)), dma((nz,)), dma((nz,)), dma((3,)),
         ],
         compiler_params=pltpu.CompilerParams(
@@ -390,6 +394,14 @@
         ),
         name="layer",
     )(tokens, routes.T, keep, router.T, w_gate, w_up, w_down)
+    out = pl.pallas_call(
+        store,
+        out_shape=tuple(jax.ShapeDtypeStruct(*s) for s in shapes),
+        in_specs=[pl.BlockSpec(memory_space=vmem)] * 4,
+        out_specs=(anywhere,) * 4,
+        scratch_shapes=[dma((4,))],
+        name="store",
+    )(*(pltpu.with_memory_space_constraint(h, vmem) for h in held))
     return out[0], out[1], out[2], out[3].T
 
 

time: 137 us -> 107 us (0.78)
  Pallas kernels: 131 us -> 106 us
  local copies, waits for them, and re-layouts: 6.01 us -> 0 us
    pallas_call x1, Pallas kernels: 131 us -> 105 us  [layer(): pl.pallas_call(functools.partial(kernel, nz, rows, cols, hid), out_shape=...]
    unnamed x4 -> x0, local copies, waits for them, and re-layouts: 6.01 us -> none
where the time goes in v2:
time: 107 us
  Pallas kernels  106 us (99%)
    pallas_call x1, Pallas kernels, layer(): pl.pallas_call(functools.partial(kernel, nz, rows, cols, hid), out_shape=...  105 us

profile of v2, /device:TPU:1, one launch (start us, length us, event | category | flops | bytes accessed | tf_op | source)
XLA Modules:
  0.0 106.9 jit_solution(821876125715405553)
XLA Ops:
  0.6 105.5 %layer.1 = (bf16[128,384]{1,0:T(8,128)(2,1)S(1)}, bf16[128,384]{1,0:T(8,128)(2,1)S(1)}, f32[128,384]{1,0:T(8,128)S(1)}, f32[8,384]{1,0:T(8,128)S(1)}) custom-call(bf16[128,384]{1,0:T(8,128)(2,1)} %tok_hbm.1, s32[2,128]{1,0:T(2,128)} %bitcast.4, s32[1,8]{1,0:T(1,128)} %keep_hbm.1, f32[8,384]{1,0:T(8,128)} %bitcast.3, bf16[1,6144,256]{2,1,0:T(8,128)(2,1)} %wg_hbm.1, ...), custom_call_target="tpu_custom_call" | custom-call | tf_op jit(solution)/shard_map/layer/pallas_call | solution.py:372
  106.1 0.8 store.1

commit v3 on v2

--- a/solution.py
+++ b/solution.py
@@ -18,11 +18,11 @@
     nz, rows, cols, hid, tok_hbm, routes_hbm, keep_hbm, router_hbm, wg_hbm, wu_hbm, wd_hbm,
     full_v, pruned_v, resid_v, grad_v,
     tok, routes, keep, router, wg, wu, wd,
-    X, lhs, T, Q, R0, RA1, RA2, RB1, RB2, out, ret,
+    X0, X1, YS, lhs, T, Q, R0, RA1, RA2, RB1, RB2, RL, out, ret,
     LD, LI, LG, stat,
-    in_sem, zin_sem, s1_sem, s1h_sem, s2_sem, s2h_sem, xx_sem, pp_sem,
-    a1_sem, a2_sem, b1_sem, b2_sem, ret_sem, small_sem,
-    send_ag, send_rs, send_x, send_p, send_z, send_r, send_small,
+        in_sem, zin_sem, zf_sem, s1_sem, s1h_sem, s2_sem, s2h_sem, xx_sem, pp_sem,
+    a1_sem, a2_sem, b1_sem, b2_sem, rl_sem, ret_sem, small_sem,
+    send_ag, send_ra, send_rb, send_rl, send_x, send_p, send_z, send_zf, send_r, send_small,
 ):
     f32, bf16 = jnp.float32, jnp.bfloat16
     d = lax.axis_index("dp")
@@ -67,6 +67,12 @@
         q = (me + j) % nq
         pl.semaphore_signal(barrier, inc=1, device_id={"dp": q // nz, "expert": q % nz}, device_id_type=MESH)
 
+    for a1 in range(1, RING):
+        for step in (1, nz - 1):
+            pl.semaphore_signal(
+                barrier, inc=1, device_id={"ffn": place(a1, 0), "expert": (z + step) % nz}, device_id_type=MESH
+            )
+
     loads = [
         pltpu.make_async_copy(routes_hbm, routes, in_sem.at[0]),
         pltpu.make_async_copy(tok_hbm, tok, in_sem.at[1]),
@@ -75,6 +81,8 @@
         pltpu.make_async_copy(wg_hbm.at[0], wg, in_sem.at[4]),
         pltpu.make_async_copy(wu_hbm.at[0], wu, in_sem.at[5]),
         pltpu.make_async_copy(wd_hbm.at[0], wd, in_sem.at[6]),
+        pltpu.make_async_copy(tok_hbm.at[pl.ds(0, rows)], X0.at[nz, f], in_sem.at[7]),
+        pltpu.make_async_copy(tok_hbm.at[pl.ds(rows, rows)], X0.at[nz + 1, f], in_sem.at[8]),
     ]
     for load in loads:
         load.start()
@@ -94,78 +102,90 @@
 
     loads[1].wait()
     slot = lax.broadcasted_iota(jnp.int32, (rows, toks), 0)
-    for k in range(nz):
-        e = (z + nz - k) % nz
+
+    def picks(e):
         at = (slot + e * rows).astype(f32)
-        pick = jnp.logical_or(at == pos0, at == pos1).astype(f32).astype(bf16)
-        picked = jnp.dot(pick, tok[...], preferred_element_type=f32).astype(bf16)
-        if k == 0:
-            X[0, 0, f] = picked
-        else:
-            out[k] = picked
-    pl.semaphore_wait(barrier, PLANE - 1 + nq - 1)
-    for k in range(1, nz):
-        send(out.at[k], X.at[0, k, f], send_z.at[k], zin_sem.at[k], {"expert": (z + nz - k) % nz})
+        return jnp.logical_or(at == pos0, at == pos1).astype(f32).astype(bf16)
+
+    def away(c):
+        far = jnp.where(c == nz - 2, 1, jnp.where(c == nz - 1, nz - 1, c + 1))
+        return jnp.where(c == 0, 0, far)
+
+    for c in range(1, nz - 2):
+        out[c] = jnp.dot(picks((z + nz - c - 1) % nz), tok[...], preferred_element_type=f32).astype(bf16)
+    loads[7].wait()
+    loads[8].wait()
+    pl.semaphore_wait(barrier, PLANE - 1 + nq - 1 + 2 * (RING - 1))
+    for c in range(1, nz - 2):
+        send(out.at[c], X0.at[c, f], send_z, zin_sem.at[c], {"expert": (z + nz - c - 1) % nz})
+
+    def share_own(k, m):
+        own = X0.at[k, f]
+        send(own, own, send_ag, s1_sem.at[m], plane(up1))
+        send(own, own, send_ag, s1_sem.at[m], plane(dn1))
+        send(own, own, send_ag, s2_sem.at[m, 0], plane(up2))
+        send(own, own, send_ag, s2_sem.at[m, 0], plane(dn2))
 
     def ag_a(k):
-        @pl.when(k > 0)
-        def _():
-            landed(X.at[0, k, f], zin_sem.at[k])
-
-        own = X.at[0, k, f]
-        send(own, own, send_ag.at[k], s1_sem.at[k, 0], plane(up1))
-        send(own, own, send_ag.at[k], s1_sem.at[k, 1], plane(dn1))
-        send(own, own, send_ag.at[k], s2_sem.at[k, 0, 0], plane(up2))
-        send(own, own, send_ag.at[k], s2_sem.at[k, 1, 0], plane(dn2))
+        landed(X0.at[k, f], zin_sem.at[k])
+        share_own(k, k)
 
     lo, hi = pl.ds(0, half), pl.ds(half, half)
 
-    def across(k, p, r):
-        ref = X.at[0, k, p]
-        send(ref, ref, send_ag.at[k], s2_sem.at[k, 0, r], plane(up2))
-        send(ref, ref, send_ag.at[k], s2_sem.at[k, 1, r], plane(dn2))
-
-    def ag_b(k):
-        landed(X.at[0, k, dn1], s1_sem.at[k, 0])
-        send(X.at[0, k, dn1, lo], X.at[0, k, dn1, lo], send_ag.at[k], s1h_sem.at[k, 0], plane(up1))
-        across(k, dn1, 1)
-        landed(X.at[0, k, up1], s1_sem.at[k, 1])
-        send(X.at[0, k, up1, hi], X.at[0, k, up1, hi], send_ag.at[k], s1h_sem.at[k, 1], plane(dn1))
-        across(k, up1, 2)
-
-    def ag_c(k):
-        op1 = place(2, 0)
-        landed(X.at[0, k, op1, lo], s1h_sem.at[k, 0])
-        landed(X.at[0, k, op1, hi], s1h_sem.at[k, 1])
-        across(k, op1, 3)
-
-    turns = (0, 3, 1, 2)
-
-    def ag_d(k, which=(0, 1, 2)):
-        for r in which:
-            a1 = turns[r]
-            p = place(a1, 3)
-            landed(X.at[0, k, p], s2_sem.at[k, 0, r])
-            send(X.at[0, k, p, lo], X.at[0, k, p, lo], send_ag.at[k], s2h_sem.at[k, 0, r], plane(up2))
-            p = place(a1, 1)
-            landed(X.at[0, k, p], s2_sem.at[k, 1, r])
-            send(X.at[0, k, p, hi], X.at[0, k, p, hi], send_ag.at[k], s2h_sem.at[k, 1, r], plane(dn2))
-
-    def ag_d3(k):
-        ag_d(k, (3,))
-
-    def ag_e(k):
-        for r, a1 in enumerate(turns):
-            p = place(a1, 2)
-            landed(X.at[0, k, p, lo], s2h_sem.at[k, 0, r])
-            landed(X.at[0, k, p, hi], s2h_sem.at[k, 1, r])
-        send(X.at[0, k], X.at[1, k], send_x.at[k], xx_sem.at[k], {"dp": 1 - d})
+    def across(k, m, p, r):
+        ref = X0.at[k, p]
+        send(ref, ref, send_ag, s2_sem.at[m, r], plane(up2))
+        send(ref, ref, send_ag, s2_sem.at[m, r], plane(dn2))
+
+    def ag_b(k, m):
+        landed(X0.at[k, pl.ds(0, 2)], s1_sem.at[m])
+        send(X0.at[k, dn1, lo], X0.at[k, dn1, lo], send_ag, s1h_sem.at[m], plane(up1))
+        send(X0.at[k, up1, hi], X0.at[k, up1, hi], send_ag, s1h_sem.at[m], plane(dn1))
+        across(k, m, dn1, 1)
+        across(k, m, up1, 1)
+
+    def ag_c(k, m):
+        landed(X0.at[k, 0], s1h_sem.at[m])
+        across(k, m, place(2, 0), 2)
+
+    def ag_d(k, m, r, turns):
+        landed(X0.at[k, pl.ds(0, 2 * len(turns))], s2_sem.at[m, r])
+        for a1 in turns:
+            p, q = place(a1, 3), place(a1, 1)
+            send(X0.at[k, p, lo], X0.at[k, p, lo], send_ag, s2h_sem.at[m], plane(up2))
+            send(X0.at[k, q, hi], X0.at[k, q, hi], send_ag, s2h_sem.at[m], plane(dn2))
+
+    def ag_d0(k, m):
+        ag_d(k, m, 0, (0,))
+        ag_d(k, m, 1, (3, 1))
+
+    def ag_d3(k, m):
+        ag_d(k, m, 2, (2,))
+
+    def to_sibling(k):
+        send(X0.at[k], X1.at[k], send_x, xx_sem.at[k], {"dp": 1 - d})
+
+    def ag_e(k, m):
+        landed(X0.at[k, pl.ds(0, RING)], s2h_sem.at[m])
+
+    def dispatch():
+        below, above = (z + nz - 1) % nz, (z + 1) % nz
+        pick = jnp.concatenate([picks(z), picks(below), picks(above)], axis=0)
+        for s in range(PLANE):
+            both = jnp.concatenate([X0[nz, s], X0[nz + 1, s]], axis=0)
+            picked = jnp.dot(pick, both, preferred_element_type=f32).astype(bf16)
+            X0[0, s] = picked[0:rows]
+            YS[0, s] = picked[rows:2 * rows]
+            YS[1, s] = picked[2 * rows:]
+        send(YS.at[0], X0.at[nz - 2], send_zf, zf_sem.at[0], {"expert": below})
+        send(YS.at[1], X0.at[nz - 1], send_zf, zf_sem.at[1], {"expert": above})
+        to_sibling(0)
 
     def work(k):
-        landed(X.at[1, k], xx_sem.at[k])
-        for c in range(2):
+        landed(X1.at[k], xx_sem.at[k])
+        for c, source in enumerate((X0, X1)):
             for s in range(PLANE):
-                lhs[c * rows:(c + 1) * rows, s * cols:(s + 1) * cols] = X[c, k, s]
+                lhs[c * rows:(c + 1) * rows, s * cols:(s + 1) * cols] = source[k, s]
         gate = jnp.dot(lhs[...], wg[...], preferred_element_type=f32)
         up = jnp.dot(lhs[...], wu[...], preferred_element_type=f32)
         hidden = (gate / (1.0 + jnp.exp(-gate)) * up).astype(bf16)
@@ -174,7 +194,7 @@
             for t in range(2):
                 T[k, s + t] = part[0:rows, t * cols:(t + 1) * cols]
                 Q[k, s + t] = part[rows:, t * cols:(t + 1) * cols]
-        send(Q.at[k], R0.at[k], send_p.at[k], pp_sem.at[k], {"dp": 1 - d})
+        send(Q.at[k], R0.at[k], send_p, pp_sem.at[k], {"dp": 1 - d})
 
     order = (2, 1, 3, 0)
 
@@ -183,8 +203,9 @@
 
         def across_1(a1):
             p = place(a1, 2)
-            send(T.at[k, p, lo], RA1.at[k, 0, a1], send_rs.at[k], a1_sem.at[k, 0, a1], plane(up2))
-            send(T.at[k, p, hi], RA1.at[k, 1, a1], send_rs.at[k], a1_sem.at[k, 1, a1], plane(dn2))
+            g = 0 if a1 == order[0] else 1
+            send(T.at[k, p, lo], RA1.at[k, 0, a1], send_ra, a1_sem.at[k, g], plane(up2))
+            send(T.at[k, p, hi], RA1.at[k, 1, a1], send_ra, a1_sem.at[k, g], plane(dn2))
 
         held = None
         for a2 in (2, 1, 3, 0):
@@ -196,43 +217,49 @@
                 held = a1 if a2 == 2 else None
 
     def rs_2(k):
-        held = None
-        for a1 in order:
-            p, q = place(a1, 1), place(a1, 3)
-            landed(RA1.at[k, 0, a1], a1_sem.at[k, 0, a1])
-            T[k, p, lo] = T[k, p, lo] + RA1[k, 0, a1]
-            if held is not None:
-                send(T.at[k, place(held, 3)], RA2.at[k, 1, held], send_rs.at[k], a2_sem.at[k, 1, held], plane(dn2))
-            landed(RA1.at[k, 1, a1], a1_sem.at[k, 1, a1])
-            T[k, q, hi] = T[k, q, hi] + RA1[k, 1, a1]
-            send(T.at[k, p], RA2.at[k, 0, a1], send_rs.at[k], a2_sem.at[k, 0, a1], plane(up2))
-            held = a1
-        send(T.at[k, place(held, 3)], RA2.at[k, 1, held], send_rs.at[k], a2_sem.at[k, 1, held], plane(dn2))
+        for g, turns in enumerate((order[:1], order[1:])):
+            landed(RA1.at[k, :, pl.ds(0, len(turns))], a1_sem.at[k, g])
+            for a1 in turns:
+                p, q = place(a1, 1), place(a1, 3)
+                T[k, p, lo] = T[k, p, lo] + RA1[k, 0, a1]
+                T[k, q, hi] = T[k, q, hi] + RA1[k, 1, a1]
+            for a1 in turns:
+                send(T.at[k, place(a1, 1)], RA2.at[k, 0, a1], send_ra, a2_sem.at[k, g], plane(up2))
+                send(T.at[k, place(a1, 3)], RA2.at[k, 1, a1], send_ra, a2_sem.at[k, g], plane(dn2))
 
     def total(own, one, two):
         return (own.astype(f32) + one.astype(f32) + two.astype(f32)).astype(bf16)
 
     def rs_3(k):
-        for a1 in order:
-            landed(RA2.at[k, 0, a1], a2_sem.at[k, 0, a1])
-            landed(RA2.at[k, 1, a1], a2_sem.at[k, 1, a1])
-            p = place(a1, 0)
-            T[k, p] = total(T[k, p], RA2[k, 0, a1], RA2[k, 1, a1])
-            if a1 == order[0]:
-                send(T.at[k, p, lo], RB1.at[k, 0], send_rs.at[k], b1_sem.at[k, 0], plane(up1))
-                send(T.at[k, p, hi], RB1.at[k, 1], send_rs.at[k], b1_sem.at[k, 1], plane(dn1))
+        home = (z + away(k)) % nz
+        for g, turns in enumerate((order[:1], order[1:])):
+            landed(RA2.at[k, :, pl.ds(0, len(turns))], a2_sem.at[k, g])
+            for a1 in turns:
+                p = place(a1, 0)
+                T[k, p] = total(T[k, p], RA2[k, 0, a1], RA2[k, 1, a1])
+
+            @pl.when(k >= nz - 2)
+            def _():
+                for a1 in turns:
+                    p = place(a1, 0)
+                    send(T.at[k, p], RL.at[k - (nz - 2), a1], send_rl, rl_sem, {"ffn": p, "expert": home})
+
+            if g == 0:
+                @pl.when(k < nz - 2)
+                def _():
+                    p = place(order[0], 0)
+                    send(T.at[k, p, lo], RB1.at[k, 0], send_rb, b1_sem.at[k], plane(up1))
+                    send(T.at[k, p, hi], RB1.at[k, 1], send_rb, b1_sem.at[k], plane(dn1))
 
     def rs_4(k):
-        landed(RB1.at[k, 0], b1_sem.at[k, 0])
+        landed(RB1.at[k], b1_sem.at[k])
         T[k, up1, lo] = T[k, up1, lo] + RB1[k, 0]
-        send(T.at[k, up1], RB2.at[k, 0], send_rs.at[k], b2_sem.at[k, 0], plane(up1))
-        landed(RB1.at[k, 1], b1_sem.at[k, 1])
         T[k, dn1, hi] = T[k, dn1, hi] + RB1[k, 1]
-        send(T.at[k, dn1], RB2.at[k, 1], send_rs.at[k], b2_sem.at[k, 1], plane(dn1))
+        send(T.at[k, up1], RB2.at[k, 0], send_rb, b2_sem.at[k], plane(up1))
+        send(T.at[k, dn1], RB2.at[k, 1], send_rb, b2_sem.at[k], plane(dn1))
 
     def rs_5(k):
-        landed(RB2.at[k, 0], b2_sem.at[k, 0])
-        landed(RB2.at[k, 1], b2_sem.at[k, 1])
+        landed(RB2.at[k], b2_sem.at[k])
         summed = total(T[k, f], RB2[k, 0], RB2[k, 1])
 
         @pl.when(k == 0)
@@ -242,7 +269,7 @@
         @pl.when(k > 0)
         def _():
             T[k, f] = summed
-            send(T.at[k, f], ret.at[z], send_r.at[k], ret_sem.at[k], {"expert": (z + k) % nz})
+            send(T.at[k, f], ret.at[z], send_r, ret_sem, {"expert": (z + away(k)) % nz})
 
     def logits_out():
         loads[3].wait()
@@ -254,20 +281,56 @@
         for j in range(1, PLANE):
             send(LD.at[f], LD.at[f], send_small.at[0], small_sem.at[0], plane((f + j) % PLANE))
 
-    def when(k, stage):
-        @pl.when(jnp.logical_and(k >= 0, k < nz))
+    def when(k, stage, end=nz):
+        @pl.when(jnp.logical_and(k >= 0, k < end))
         def _():
             stage(k)
 
-    @pl.loop(0, nz + LAG + 4)
+    def gather(k, stage):
+        @pl.when(k == 0)
+        def _():
+            for j in range(2):
+                stage(nz + j, j * (nz - 2))
+
+        @pl.when(jnp.logical_and(k >= 1, k < nz - 2))
+        def _():
+            stage(k, k)
+
+    def chunk(k, stage):
+        @pl.when(jnp.logical_and(k >= 1, k < nz - 2))
+        def _():
+            stage(k)
+
+    def ready(k):
+        gather(k, ag_e)
+        chunk(k, to_sibling)
+
+        @pl.when(k == 0)
+        def _():
+            dispatch()
+
+        @pl.when(jnp.logical_and(k >= nz - 2, k < nz))
+        def _():
+            landed(X0.at[k], zf_sem.at[k - nz + 2])
+            to_sibling(k)
+
+    for j in range(2):
+        share_own(nz + j, j * (nz - 2))
+
+    @pl.loop(1, nz + LAG + 2)
     def _(i):
-        when(i - 1, ag_b)
-        when(i - 2, ag_c)
-        when(i - 2, ag_d)
-        when(i - 3, ag_d3)
-        when(i - 4, ag_e)
-        when(2 * i - 1, ag_a)
-        when(2 * i, ag_a)
+        gather(jnp.where(i == 2, -1, i - 1), ag_b)
+        gather(i - 2, ag_c)
+        gather(i - 2, ag_d0)
+
+        @pl.when(i == 2)
+        def _():
+            ag_b(1, 1)
+
+        gather(i - 3, ag_d3)
+        ready(i - 4)
+        chunk(2 * i - 1, ag_a)
+        chunk(2 * i, ag_a)
 
         @pl.when(i == 1)
         def _():
@@ -283,8 +346,8 @@
         when(i - LAG, rs_1)
         when(i - LAG - 1, rs_2)
         when(i - LAG - 2, rs_3)
-        when(i - LAG - 3, rs_4)
-        when(i - LAG - 4, rs_5)
+        when(i - LAG - 3, rs_4, nz - 2)
+        when(i - LAG - 4, rs_5, nz - 2)
 
     loads[2].wait()
     landed(LD.at[pl.ds(0, PLANE - 1)], small_sem.at[0])
@@ -306,8 +369,11 @@
     pruned0 = k0 * (k1 * share + 1.0 - k1)
     pruned1 = k1 * (k0 * other + 1.0 - k0)
 
-    for k in range(1, nz):
-        landed(ret.at[k], ret_sem.at[k])
+    landed(ret.at[pl.ds(0, nz - 3)], ret_sem)
+    landed(RL, rl_sem)
+    for j, step in enumerate((nz - 1, 1)):
+        terms = RL[j].astype(f32)
+        ret[(z + step) % nz] = (terms[0] + terms[1] + terms[2] + terms[3]).astype(bf16)
     returned = ret[...].reshape(nz * rows, cols)
     first = jnp.dot(pick0, returned, preferred_element_type=f32)
     second = jnp.dot(pick1, returned, preferred_element_type=f32)
@@ -324,16 +390,15 @@
     share_row = 1.0 / (1.0 + jnp.exp(-diff))
     rate = share_row * (1.0 - share_row) * (1.0 - keep0 * keep1)
     sent(LD.at[pl.ds(0, PLANE - 1)], send_small.at[0])
-    @pl.loop(0, nz)
-    def _(k):
-        sent(X.at[0, k, pl.ds(0, 15)], send_ag.at[k])
-        sent(T.at[k, pl.ds(0, 15)], send_rs.at[k])
-        sent(X.at[0, k], send_x.at[k])
-        sent(Q.at[k], send_p.at[k])
-
-    for k in range(1, nz):
-        sent(out.at[k], send_z.at[k])
-        sent(T.at[k, f], send_r.at[k])
+    sent(X0.at[pl.ds(0, nz - 1), pl.ds(0, PLANE - 1)], send_ag)
+    sent(T.at[:, pl.ds(0, 3 * RING)], send_ra)
+    sent(T.at[pl.ds(0, nz - 2), pl.ds(0, 3)], send_rb)
+    sent(RL, send_rl)
+    sent(X1, send_x)
+    sent(YS, send_zf)
+    sent(Q, send_p)
+    sent(out.at[pl.ds(0, nz - 3)], send_z)
+    sent(out.at[pl.ds(0, nz - 3)], send_r)
     landed(LI.at[pl.ds(0, PLANE - 1)], small_sem.at[1])
     inner = jnp.sum(LI[...], axis=0)[0:1]
     slope = rate * inner
@@ -377,17 +442,17 @@
         scratch_shapes=[
             vmem((toks, cols), bf16), vmem((2, toks), jnp.int32), vmem((1, nz), jnp.int32), vmem((nz, cols), f32),
             vmem((depth, hid), bf16), vmem((depth, hid), bf16), vmem((hid, depth), bf16),
-            vmem((2, nz, PLANE, *shard), bf16), vmem((toks, depth), bf16),
+            vmem((nz + 2, PLANE, *shard), bf16), vmem((nz, PLANE, *shard), bf16), vmem((2, PLANE, *shard), bf16),
+            vmem((toks, depth), bf16),
             vmem((nz, PLANE, *shard), bf16), vmem((nz, PLANE, *shard), bf16), vmem((nz, PLANE, *shard), bf16),
             vmem((nz, 2, RING, *piece), bf16), vmem((nz, 2, RING, *shard), bf16),
-            vmem((nz, 2, *piece), bf16), vmem((nz, 2, *shard), bf16),
+            vmem((nz - 2, 2, *piece), bf16), vmem((nz - 2, 2, *shard), bf16), vmem((2, RING, *shard), bf16),
             vmem((nz, *shard), bf16), vmem((nz, *shard), bf16),
             vmem((PLANE, 8, toks), f32), vmem((PLANE, 8, toks), f32), vmem((nq, nz, cols), bf16),
             vmem((128, toks), f32),
-            dma((7,)), dma((nz,)), dma((nz, 2)), dma((nz, 2)), dma((nz, 2, RING)), dma((nz, 2, RING)),
-            dma((nz,)), dma((nz,)),
-            dma((nz, 2, RING)), dma((nz, 2, RING)), dma((nz, 2)), dma((nz, 2)), dma((nz,)), dma((3,)),
-            dma((nz,)), dma((nz,)), dma((nz,)), dma((nz,)), dma((nz,)), dma((nz,)), dma((3,)),
+            dma((9,)), dma((nz,)), dma((2,)), dma((nz,)), dma((nz,)), dma((nz, 3)), dma((nz,)), dma((nz,)), dma((nz,)),
+            dma((nz, 2)), dma((nz, 2)), dma((nz - 2,)), dma((nz - 2,)), dma, dma, dma((3,)),
+            dma, dma, dma, dma, dma, dma, dma, dma, dma, dma((3,)),
         ],
         compiler_params=pltpu.CompilerParams(
             collective_id=0, has_side_effects=True, vmem_limit_bytes=60 * 1024 * 1024

time: 107 us -> 102 us (0.953)
  Pallas kernels: 106 us -> 101 us
    pallas_call x1, Pallas kernels: 105 us -> 100 us  [layer(): pl.pallas_call(functools.partial(kernel, nz, rows, cols, hid), out_shape=...]
where the time goes in v3:
time: 102 us
  Pallas kernels  101 us (99%)
    pallas_call x1, Pallas kernels, layer(): pl.pallas_call(functools.partial(kernel, nz, rows, cols, hid), out_shape=...  100 us

profile of v3, /device:TPU:1, one launch (start us, length us, event | category | flops | bytes accessed | tf_op | source)
XLA Modules:
  0.0 101.8 jit_solution(7578504452056998294)
XLA Ops:
  0.6 100.4 %layer.1 = (bf16[128,384]{1,0:T(8,128)(2,1)S(1)}, bf16[128,384]{1,0:T(8,128)(2,1)S(1)}, f32[128,384]{1,0:T(8,128)S(1)}, f32[8,384]{1,0:T(8,128)S(1)}) custom-call(bf16[128,384]{1,0:T(8,128)(2,1)} %tok_hbm.1, s32[2,128]{1,0:T(2,128)} %bitcast.4, s32[1,8]{1,0:T(1,128)} %keep_hbm.1, f32[8,384]{1,0:T(8,128)} %bitcast.3, bf16[1,6144,256]{2,1,0:T(8,128)(2,1)} %wg_hbm.1, ...), custom_call_target="tpu_custom_call" | custom-call | tf_op jit(solution)/shard_map/layer/pallas_call | solution.py:437
  101.1 0.8 store.1

commit v4 on v3

--- a/solution.py
+++ b/solution.py
@@ -22,7 +22,7 @@
     LD, LI, LG, stat,
         in_sem, zin_sem, zf_sem, s1_sem, s1h_sem, s2_sem, s2h_sem, xx_sem, pp_sem,
     a1_sem, a2_sem, b1_sem, b2_sem, rl_sem, ret_sem, small_sem,
-    send_ag, send_ra, send_rb, send_rl, send_x, send_p, send_z, send_zf, send_r, send_small,
+    send_ag, send_ra, send_rb, send_rl, send_x, send_p, send_z, send_zf, send_r, send_small, hop_sem,
 ):
     f32, bf16 = jnp.float32, jnp.bfloat16
     d = lax.axis_index("dp")
@@ -61,17 +61,10 @@
         return {"ffn": p}
 
     barrier = pltpu.get_barrier_semaphore()
-    for j in range(1, PLANE):
-        pl.semaphore_signal(barrier, inc=1, device_id={"ffn": (f + j) % PLANE}, device_id_type=MESH)
-    for j in range(1, nq):
-        q = (me + j) % nq
-        pl.semaphore_signal(barrier, inc=1, device_id={"dp": q // nz, "expert": q % nz}, device_id_type=MESH)
-
-    for a1 in range(1, RING):
-        for step in (1, nz - 1):
-            pl.semaphore_signal(
-                barrier, inc=1, device_id={"ffn": place(a1, 0), "expert": (z + step) % nz}, device_id_type=MESH
-            )
+    above, below = (z + 1) % nz, (z + nz - 1) % nz
+    beside = [plane(up1), plane(dn1), plane(up2), plane(dn2), {"dp": 1 - d}, {"expert": above}, {"expert": below}]
+    for device in beside:
+        pl.semaphore_signal(barrier, inc=1, device_id=device, device_id_type=MESH)
 
     loads = [
         pltpu.make_async_copy(routes_hbm, routes, in_sem.at[0]),
@@ -84,8 +77,8 @@
         pltpu.make_async_copy(tok_hbm.at[pl.ds(0, rows)], X0.at[nz, f], in_sem.at[7]),
         pltpu.make_async_copy(tok_hbm.at[pl.ds(rows, rows)], X0.at[nz + 1, f], in_sem.at[8]),
     ]
-    for load in loads:
-        load.start()
+    for j in (0, 7, 8, 1, 2, 3, 4, 5, 6):
+        loads[j].start()
 
     loads[0].wait()
     r0 = routes[0:1, :]
@@ -108,17 +101,10 @@
         return jnp.logical_or(at == pos0, at == pos1).astype(f32).astype(bf16)
 
     def away(c):
-        far = jnp.where(c == nz - 2, 1, jnp.where(c == nz - 1, nz - 1, c + 1))
-        return jnp.where(c == 0, 0, far)
+        return jnp.where(c == 0, 0, c + 1)
 
     for c in range(1, nz - 2):
         out[c] = jnp.dot(picks((z + nz - c - 1) % nz), tok[...], preferred_element_type=f32).astype(bf16)
-    loads[7].wait()
-    loads[8].wait()
-    pl.semaphore_wait(barrier, PLANE - 1 + nq - 1 + 2 * (RING - 1))
-    for c in range(1, nz - 2):
-        send(out.at[c], X0.at[c, f], send_z, zin_sem.at[c], {"expert": (z + nz - c - 1) % nz})
-
     def share_own(k, m):
         own = X0.at[k, f]
         send(own, own, send_ag, s1_sem.at[m], plane(up1))
@@ -169,7 +155,6 @@
         landed(X0.at[k, pl.ds(0, RING)], s2h_sem.at[m])
 
     def dispatch():
-        below, above = (z + nz - 1) % nz, (z + 1) % nz
         pick = jnp.concatenate([picks(z), picks(below), picks(above)], axis=0)
         for s in range(PLANE):
             both = jnp.concatenate([X0[nz, s], X0[nz + 1, s]], axis=0)
@@ -177,8 +162,9 @@
             X0[0, s] = picked[0:rows]
             YS[0, s] = picked[rows:2 * rows]
             YS[1, s] = picked[2 * rows:]
-        send(YS.at[0], X0.at[nz - 2], send_zf, zf_sem.at[0], {"expert": below})
-        send(YS.at[1], X0.at[nz - 1], send_zf, zf_sem.at[1], {"expert": above})
+        for j, part in enumerate((lo, hi)):
+            send(YS.at[0, :, part], X0.at[nz - 2 + j, :, lo], send_zf, zf_sem.at[j], {"expert": below})
+            send(YS.at[1, :, part], X0.at[nz - 2 + j, :, hi], send_zf, zf_sem.at[j], {"expert": above})
         to_sibling(0)
 
     def work(k):
@@ -231,7 +217,6 @@
         return (own.astype(f32) + one.astype(f32) + two.astype(f32)).astype(bf16)
 
     def rs_3(k):
-        home = (z + away(k)) % nz
         for g, turns in enumerate((order[:1], order[1:])):
             landed(RA2.at[k, :, pl.ds(0, len(turns))], a2_sem.at[k, g])
             for a1 in turns:
@@ -242,7 +227,8 @@
             def _():
                 for a1 in turns:
                     p = place(a1, 0)
-                    send(T.at[k, p], RL.at[k - (nz - 2), a1], send_rl, rl_sem, {"ffn": p, "expert": home})
+                    send(T.at[k, p, lo], RL.at[0, k - (nz - 2), a1], send_rl, rl_sem, {"ffn": p, "expert": above})
+                    send(T.at[k, p, hi], RL.at[1, k - (nz - 2), a1], send_rl, rl_sem, {"ffn": p, "expert": below})
 
             if g == 0:
                 @pl.when(k < nz - 2)
@@ -277,7 +263,7 @@
             router[...], tok[...].astype(f32), (((1,), (1,)), ((), ())), precision=HIGH, preferred_element_type=f32
         )
         part = jnp.sum(local * (oh0 - oh1), axis=0, keepdims=True)
-        LD[f] = jnp.broadcast_to(part, (8, toks))
+        LD[f] = part
         for j in range(1, PLANE):
             send(LD.at[f], LD.at[f], send_small.at[0], small_sem.at[0], plane((f + j) % PLANE))
 
@@ -314,8 +300,18 @@
             landed(X0.at[k], zf_sem.at[k - nz + 2])
             to_sibling(k)
 
+    loads[7].wait()
+    loads[8].wait()
+    pl.semaphore_wait(barrier, len(beside))
     for j in range(2):
         share_own(nz + j, j * (nz - 2))
+
+    for reach in range(2, nz // 2 + 1):
+        for step in (above, below):
+            pl.semaphore_signal(hop_sem.at[reach - 2], inc=1, device_id={"expert": step}, device_id_type=MESH)
+        pl.semaphore_wait(hop_sem.at[reach - 2], 2)
+        for c in sorted({reach - 1, nz - reach - 1}):
+            send(out.at[c], X0.at[c, f], send_z, zin_sem.at[c], {"expert": (z + nz - c - 1) % nz})
 
     @pl.loop(1, nz + LAG + 2)
     def _(i):
@@ -332,12 +328,9 @@
         chunk(2 * i - 1, ag_a)
         chunk(2 * i, ag_a)
 
-        @pl.when(i == 1)
+        @pl.when(i == 5)
         def _():
             logits_out()
-
-        @pl.when(i == 5)
-        def _():
             loads[4].wait()
             loads[5].wait()
             loads[6].wait()
@@ -351,7 +344,7 @@
 
     loads[2].wait()
     landed(LD.at[pl.ds(0, PLANE - 1)], small_sem.at[0])
-    diff = jnp.sum(LD[...], axis=0)[0:1]
+    diff = jnp.sum(LD[...], axis=0)
     wide = jnp.broadcast_to(keep[...].astype(f32), (nz, nz))
     diagonal = lax.broadcasted_iota(jnp.int32, (nz, nz), 0) == lax.broadcasted_iota(jnp.int32, (nz, nz), 1)
     keep_column = jnp.sum(jnp.where(diagonal, wide, 0.0), axis=1, keepdims=True)
@@ -372,8 +365,9 @@
     landed(ret.at[pl.ds(0, nz - 3)], ret_sem)
     landed(RL, rl_sem)
     for j, step in enumerate((nz - 1, 1)):
-        terms = RL[j].astype(f32)
-        ret[(z + step) % nz] = (terms[0] + terms[1] + terms[2] + terms[3]).astype(bf16)
+        for h in range(2):
+            terms = RL[j, h].astype(f32)
+            ret[(z + step) % nz, h * half:(h + 1) * half] = (terms[0] + terms[1] + terms[2] + terms[3]).astype(bf16)
     returned = ret[...].reshape(nz * rows, cols)
     first = jnp.dot(pick0, returned, preferred_element_type=f32)
     second = jnp.dot(pick1, returned, preferred_element_type=f32)
@@ -381,7 +375,7 @@
     pruned32 = pruned0 * first + pruned1 * second
     residual = full32 - pruned32
     inner_part = jnp.sum(residual * (first - second), axis=1, keepdims=True)
-    LI[f] = jnp.transpose(jnp.broadcast_to(inner_part, (toks, 128)))[0:8]
+    LI[f] = jnp.transpose(jnp.broadcast_to(inner_part, (toks, 128)))[0:1]
     for j in range(1, PLANE):
         send(LI.at[f], LI.at[f], send_small.at[1], small_sem.at[1], plane((f + j) % PLANE))
     full_v[...] = full32.astype(bf16)
@@ -400,7 +394,7 @@
     sent(out.at[pl.ds(0, nz - 3)], send_z)
     sent(out.at[pl.ds(0, nz - 3)], send_r)
     landed(LI.at[pl.ds(0, PLANE - 1)], small_sem.at[1])
-    inner = jnp.sum(LI[...], axis=0)[0:1]
+    inner = jnp.sum(LI[...], axis=0)
     slope = rate * inner
     LG[me] = jnp.dot(
         (oh0 - oh1) * slope, tok[...].astype(f32), precision=HIGH, preferred_element_type=f32
@@ -446,13 +440,13 @@
             vmem((toks, depth), bf16),
             vmem((nz, PLANE, *shard), bf16), vmem((nz, PLANE, *shard), bf16), vmem((nz, PLANE, *shard), bf16),
             vmem((nz, 2, RING, *piece), bf16), vmem((nz, 2, RING, *shard), bf16),
-            vmem((nz - 2, 2, *piece), bf16), vmem((nz - 2, 2, *shard), bf16), vmem((2, RING, *shard), bf16),
+            vmem((nz - 2, 2, *piece), bf16), vmem((nz - 2, 2, *shard), bf16), vmem((2, 2, RING, *piece), bf16),
             vmem((nz, *shard), bf16), vmem((nz, *shard), bf16),
-            vmem((PLANE, 8, toks), f32), vmem((PLANE, 8, toks), f32), vmem((nq, nz, cols), bf16),
+            vmem((PLANE, 1, toks), f32), vmem((PLANE, 1, toks), f32), vmem((nq, nz, cols), bf16),
             vmem((128, toks), f32),
             dma((9,)), dma((nz,)), dma((2,)), dma((nz,)), dma((nz,)), dma((nz, 3)), dma((nz,)), dma((nz,)), dma((nz,)),
             dma((nz, 2)), dma((nz, 2)), dma((nz - 2,)), dma((nz - 2,)), dma, dma, dma((3,)),
-            dma, dma, dma, dma, dma, dma, dma, dma, dma, dma((3,)),
+            dma, dma, dma, dma, dma, dma, dma, dma, dma, dma((3,)), pltpu.SemaphoreType.REGULAR((3,)),
         ],
         compiler_params=pltpu.CompilerParams(
             collective_id=0, has_side_effects=True, vmem_limit_bytes=60 * 1024 * 1024

time: 102 us -> 101 us (level)
  no operation moved by 1% of the time
where the time goes in v4:
time: 101 us
  Pallas kernels  100 us (99%)
    pallas_call x1, Pallas kernels, layer(): pl.pallas_call(functools.partial(kernel, nz, rows, cols, hid), out_shape=...  99.4 us

profile of v4, /device:TPU:1, one launch (start us, length us, event | category | flops | bytes accessed | tf_op | source)
XLA Modules:
  0.0 100.8 jit_solution(13021536892992237128)
XLA Ops:
  0.6 99.4 %layer.1 = (bf16[128,384]{1,0:T(8,128)(2,1)S(1)}, bf16[128,384]{1,0:T(8,128)(2,1)S(1)}, f32[128,384]{1,0:T(8,128)S(1)}, f32[8,384]{1,0:T(8,128)S(1)}) custom-call(bf16[128,384]{1,0:T(8,128)(2,1)} %tok_hbm.1, s32[2,128]{1,0:T(2,128)} %bitcast.4, s32[1,8]{1,0:T(1,128)} %keep_hbm.1, f32[8,384]{1,0:T(8,128)} %bitcast.3, bf16[1,6144,256]{2,1,0:T(8,128)(2,1)} %wg_hbm.1, ...), custom_call_target="tpu_custom_call" | custom-call | tf_op jit(solution)/shard_map/layer/pallas_call | solution.py:431
  100.0 0.8 store.1

commit v5 on v4

--- a/solution.py
+++ b/solution.py
@@ -282,10 +282,10 @@
         def _():
             stage(k, k)
 
-    def chunk(k, stage):
+    def chunk(k, stage, *more):
         @pl.when(jnp.logical_and(k >= 1, k < nz - 2))
         def _():
-            stage(k)
+            stage(k, *more)
 
     def ready(k):
         gather(k, ag_e)
@@ -312,10 +312,13 @@
         pl.semaphore_wait(hop_sem.at[reach - 2], 2)
         for c in sorted({reach - 1, nz - reach - 1}):
             send(out.at[c], X0.at[c, f], send_z, zin_sem.at[c], {"expert": (z + nz - c - 1) % nz})
+        if reach == 2:
+            for j in range(2):
+                ag_b(nz + j, j * (nz - 2))
 
     @pl.loop(1, nz + LAG + 2)
     def _(i):
-        gather(jnp.where(i == 2, -1, i - 1), ag_b)
+        chunk(jnp.where(i == 2, -1, i - 1), ag_b, i - 1)
         gather(i - 2, ag_c)
         gather(i - 2, ag_d0)
 
@@ -325,8 +328,8 @@
 
         gather(i - 3, ag_d3)
         ready(i - 4)
+        chunk(2 * i - 2, ag_a)
         chunk(2 * i - 1, ag_a)
-        chunk(2 * i, ag_a)
 
         @pl.when(i == 5)
         def _():
@@ -335,8 +338,8 @@
             loads[5].wait()
             loads[6].wait()
 
+        when(i - LAG, rs_1)
         when(i - 5, work)
-        when(i - LAG, rs_1)
         when(i - LAG - 1, rs_2)
         when(i - LAG - 2, rs_3)
         when(i - LAG - 3, rs_4, nz - 2)

time: 101 us -> 98 us (0.970)
  Pallas kernels: 100 us -> 97.3 us
    pallas_call x1, Pallas kernels: 99.4 us -> 96.5 us  [layer(): pl.pallas_call(functools.partial(kernel, nz, rows, cols, hid), out_shape=...]
where the time goes in v5:
time: 98 us; the launch traced here: 97.9 us
  Pallas kernels  97.3 us (99%)
    pallas_call x1, Pallas kernels, layer(): pl.pallas_call(functools.partial(kernel, nz, rows, cols, hid), out_shape=...  96.5 us

profile of v5, /device:TPU:1, one launch (start us, length us, event | category | flops | bytes accessed | tf_op | source)
XLA Modules:
  0.0 97.9 jit_solution(13894481175605685790)
XLA Ops:
  0.6 96.5 %layer.1 = (bf16[128,384]{1,0:T(8,128)(2,1)S(1)}, bf16[128,384]{1,0:T(8,128)(2,1)S(1)}, f32[128,384]{1,0:T(8,128)S(1)}, f32[8,384]{1,0:T(8,128)S(1)}) custom-call(bf16[128,384]{1,0:T(8,128)(2,1)} %tok_hbm.1, s32[2,128]{1,0:T(2,128)} %bitcast.4, s32[1,8]{1,0:T(1,128)} %keep_hbm.1, f32[8,384]{1,0:T(8,128)} %bitcast.3, bf16[1,6144,256]{2,1,0:T(8,128)(2,1)} %wg_hbm.1, ...), custom_call_target="tpu_custom_call" | custom-call | tf_op jit(solution)/shard_map/layer/pallas_call | solution.py:434
  97.2 0.8 store.1
